TPU v7x, 32 devices: a 4x4x1 block of a 4x4x8 slice. The times are simulated.
32 devices in a mesh: dp: 1 (over z), tp: 4 (over y), fsdp: 8 (over x, core).
Axes of the slice: x: 4, y: 4, z: 1, core: 2. Of those that a mesh axis runs over, the one named last changes fastest.
The devices are a block of a 4x4x8 slice.
Arguments:
- tokens: bfloat16 [8, 2048, 4096], P(('dp', 'fsdp'))
- positions: int32 [8, 2048], P(('dp', 'fsdp'))
- valid_len: int32 [8], P(('dp', 'fsdp'))
- w_query: bfloat16 [4096, 4096], P('fsdp', 'tp')
- w_key: bfloat16 [4096, 1024], P('fsdp', 'tp')
- w_value: bfloat16 [4096, 1024], P('fsdp', 'tp')
- w_out: bfloat16 [4096, 4096], P('tp', 'fsdp')
- w_gate: bfloat16 [4096, 14336], P('fsdp', 'tp')
- w_up: bfloat16 [4096, 14336], P('fsdp', 'tp')
- w_down: bfloat16 [14336, 4096], P('tp', 'fsdp')
- norm_attn: bfloat16 [4096], replicated
- norm_mlp: bfloat16 [4096], replicated
Outputs:
- output 1: bfloat16 [8, 2048, 4096], P(('dp', 'fsdp'))
- output 2: bfloat16 [8, 2048, 8, 128], P(('dp', 'fsdp'), None, 'tp')
- output 3: bfloat16 [8, 2048, 8, 128], P(('dp', 'fsdp'), None, 'tp')
All inputs are finite; a program needn't handle non-finite values.
Results may differ from a plain program's by a relative error of at most 0.0135249.
Values are sent between devices in bfloat16 or wider.
A program may use at most 768 MiB of HBM per device.

v0:
```python
import math
import jax
import jax.numpy as jnp
from jax import lax
from jax.sharding import PartitionSpec as P

HEAD_DIM = 128
Q_BLOCK = 256
ROPE_THETA = 500000.0
NORM_EPS = 1e-5
SCORE_SCALE = HEAD_DIM ** -0.5


def rope_freqs():
    half_idx = jnp.arange(HEAD_DIM // 2, dtype=jnp.float32)
    inv_freq = jnp.power(ROPE_THETA, -2.0 * half_idx / HEAD_DIM)
    wave_len = 2.0 * math.pi / inv_freq
    smooth = (8192.0 / wave_len - 1.0) / 3.0
    blended = (1.0 - smooth) * inv_freq / 8.0 + smooth * inv_freq
    return jnp.where(wave_len < 2048.0, inv_freq, jnp.where(wave_len > 8192.0, inv_freq / 8.0, blended))


def rms_norm(values, gain_vec):
    vals_f32 = values.astype(jnp.float32)
    inv_rms = lax.rsqrt(jnp.mean(vals_f32 * vals_f32, axis=-1, keepdims=True) + NORM_EPS)
    return (vals_f32 * inv_rms * gain_vec.astype(jnp.float32)).astype(jnp.bfloat16)


def rotate(proj_val, cos_t, sin_t):
    half_dim = proj_val.shape[-1] // 2
    lead_half = proj_val[..., :half_dim]
    tail_half = proj_val[..., half_dim:]
    return jnp.concatenate([lead_half * cos_t - tail_half * sin_t, tail_half * cos_t + lead_half * sin_t], axis=-1)


def attention(q_rot, k_rot, v_cache, valid_len):
    seq_len = q_rot.shape[1]
    block_len = min(seq_len, Q_BLOCK)
    pieces = []
    for block_idx in range(seq_len // block_len):
        first_row = block_idx * block_len
        end_row = first_row + block_len
        scores = jnp.einsum('bqkgd,bskd->bkgqs', q_rot[:, first_row:end_row], k_rot[:, :end_row], preferred_element_type=jnp.float32) * SCORE_SCALE
        q_index = jnp.arange(first_row, end_row)[:, None]
        k_index = jnp.arange(end_row)[None, :]
        allowed = (k_index <= q_index)[None] & (k_index[None] < valid_len[:, None, None])
        scores = jnp.where(allowed[:, None, None], scores, -jnp.inf)
        attn_prob = jax.nn.softmax(scores, axis=-1).astype(jnp.bfloat16)
        pieces.append(jnp.einsum('bkgqs,bskd->bqkgd', attn_prob, v_cache[:, :end_row], preferred_element_type=jnp.float32).astype(jnp.bfloat16))
    return jnp.concatenate(pieces, axis=1)


def rope_attend(q_proj, k_proj, v_proj, positions, valid_len):
    batch_loc, seq_len = positions.shape
    kv_count = k_proj.shape[-1] // HEAD_DIM
    q_count = q_proj.shape[-1] // HEAD_DIM
    angles = positions.astype(jnp.float32)[:, :, None] * rope_freqs()
    cos_t = jnp.cos(angles)[:, :, None, :]
    sin_t = jnp.sin(angles)[:, :, None, :]
    q_rot = rotate(q_proj.reshape(batch_loc, seq_len, q_count, HEAD_DIM), cos_t, sin_t).astype(jnp.bfloat16)
    q_rot = q_rot.reshape(batch_loc, seq_len, kv_count, q_count // kv_count, HEAD_DIM)
    k_rot = rotate(k_proj.reshape(batch_loc, seq_len, kv_count, HEAD_DIM), cos_t, sin_t).astype(jnp.bfloat16)
    v_cache = v_proj.astype(jnp.bfloat16).reshape(batch_loc, seq_len, kv_count, HEAD_DIM)
    attn_out = attention(q_rot, k_rot, v_cache, valid_len).reshape(batch_loc, seq_len, q_count * HEAD_DIM)
    return attn_out, k_rot, v_cache


def solution(mesh):
    batch_axes = ('dp', 'fsdp')
    in_specs = (P(batch_axes, None, None), P(batch_axes, None), P(batch_axes),
                P('fsdp', 'tp'), P('fsdp', 'tp'), P('fsdp', 'tp'), P('tp', 'fsdp'),
                P('fsdp', 'tp'), P('fsdp', 'tp'), P('tp', 'fsdp'), P(None), P(None))
    out_specs = (P(batch_axes, None, None), P(batch_axes, None, 'tp', None), P(batch_axes, None, 'tp', None))

    def local_layer(tokens, positions, valid_len, w_query, w_key, w_value, w_out, w_gate, w_up, w_down, norm_attn, norm_mlp):
        h_in = rms_norm(tokens, norm_attn)
        full_q = lax.all_gather(w_query, 'fsdp', axis=0, tiled=True)
        full_k = lax.all_gather(w_key, 'fsdp', axis=0, tiled=True)
        full_v = lax.all_gather(w_value, 'fsdp', axis=0, tiled=True)
        q_proj = jnp.einsum('btd,dk->btk', h_in, full_q, preferred_element_type=jnp.float32)
        k_proj = jnp.einsum('btd,dk->btk', h_in, full_k, preferred_element_type=jnp.float32)
        v_proj = jnp.einsum('btd,dk->btk', h_in, full_v, preferred_element_type=jnp.float32)
        attn_out, k_rot, v_cache = rope_attend(q_proj, k_proj, v_proj, positions, valid_len)
        full_o = lax.all_gather(w_out, 'fsdp', axis=1, tiled=True)
        y_part = jnp.einsum('btk,kd->btd', attn_out, full_o, preferred_element_type=jnp.float32).astype(jnp.bfloat16)
        y_attn = lax.psum(y_part, 'tp')
        resid_mid = (tokens.astype(jnp.float32) + y_attn.astype(jnp.float32)).astype(jnp.bfloat16)
        h_mlp = rms_norm(resid_mid, norm_mlp)
        full_gate = lax.all_gather(w_gate, 'fsdp', axis=0, tiled=True)
        full_up = lax.all_gather(w_up, 'fsdp', axis=0, tiled=True)
        gate_val = jnp.einsum('btd,df->btf', h_mlp, full_gate, preferred_element_type=jnp.float32)
        up_val = jnp.einsum('btd,df->btf', h_mlp, full_up, preferred_element_type=jnp.float32)
        hidden_act = (jax.nn.silu(gate_val) * up_val).astype(jnp.bfloat16)
        full_down = lax.all_gather(w_down, 'fsdp', axis=1, tiled=True)
        down_part = jnp.einsum('btf,fd->btd', hidden_act, full_down, preferred_element_type=jnp.float32).astype(jnp.bfloat16)
        down_val = lax.psum(down_part, 'tp')
        hidden_out = (resid_mid.astype(jnp.float32) + down_val.astype(jnp.float32)).astype(jnp.bfloat16)
        return hidden_out, k_rot, v_cache

    return jax.shard_map(local_layer, mesh=mesh, in_specs=in_specs, out_specs=out_specs, check_vma=False)
```

profile of v0, /device:TPU:96, one launch (start us, length us, event | category | flops | bytes accessed | tf_op | source)
XLA Modules:
  0.0 1394.4 jit_solution(11030826353871672976)
XLA Ops:
  7.2 0.7 all-gather.10.cloned.1.call-update
  8.0 0.7 all-gather.8.cloned.1.call-update
  8.8 0.7 all-gather.12.cloned.1.call-update
  9.6 0.6 all-gather.14.cloned.1.call-update
  10.4 7.2 fusion
  18.5 2.8 multiply_cosine_fusion
  21.3 0.5 fusion.55
  21.8 0.4 fusion.58
  22.2 0.3 fusion.59
  22.5 0.3 fusion.60
  22.8 0.2 fusion.131
  23.4 11.4 all-gather.10.cloned.1.call-done
  34.7 4.1 copy.15
  38.8 9.0 fusion.47
  47.8 0.3 add_convert_fusion.1
  48.2 11.3 all-gather.8.cloned.1.call-done
  59.5 10.1 fusion.50
  69.6 39.1 %all-gather.12.cloned.1.call-done = bf16[4096,1024]{1,0:T(8,128)(2,1)} async-done(((bf16[512,1024]{1,0:T(8,128)(2,1)}), bf16[4096,1024]{1,0:T(8,128)(2,1)}) %all-gather.12.cloned.1.call-update) | async-done | bytes 8388624 | tf_op jit(solution)/shard_map/all_gather | solution.py:77
  108.7 11.9 copy.16
  120.6 23.9 %fusion.38 = f32[1,2048,8,128]{1,3,2,0:T(8,128)S(1)} fusion(bf16[8,128,4096]{2,1,0:T(8,128)(2,1)} %bitcast.481, bf16[1,2048,4096]{2,1,0:T(8,128)(2,1)} %param.12, f32[4096]{0:T(1024)S(1)} %convert_element_type.172, f32[2048]{0:T(1024)S(1)} %add_rsqrt_fusion.1), kind=kOutput, calls=%fused_computation.63 | convolution fusion | flops 17213423616 | bytes 33579008 | tf_op jit(solution)/shard_map/btd,dk->btk/dot_general | solution.py:80
  144.6 3.5 add_convert_fusion
  148.1 4.8 copy.17
  152.9 4.7 copy.18
  157.7 8.2 fusion.18
  165.9 6.5 fusion.20
  172.4 2.4 fusion.24
  174.8 5.7 fusion.28
  180.5 4.1 fusion.37
  184.6 3.1 fusion.44
  187.7 2.0 fusion.212
  189.7 2.2 fusion.21
  191.9 5.2 fusion.25
  197.1 1.1 fusion.43
  198.2 0.3 fusion.57
  198.5 2.3 fusion.95
  200.7 3.2 fusion.91
  204.0 8.1 fusion.17
  212.1 1.3 fusion.31
  213.4 7.1 fusion.19
  220.5 8.2 fusion.16
  228.7 3.7 fusion.123
  232.5 9.7 fusion.15
  242.3 6.9 fusion.85
  249.2 3.8 fusion.117
  253.0 9.4 fusion.111
  262.4 6.4 fusion.105
  268.8 6.7 fusion.99
  275.5 24.9 %convert_bitcast_fusion.1 = bf16[1,2048,4096]{2,1,0:T(8,128)(2,1)} fusion(bf16[2048,1024]{0,1:T(8,128)(2,1)} %bitcast.496, bf16[1024,4096]{1,0:T(8,128)(2,1)} %all-gather.14.cloned.1.call-done), kind=kOutput, calls=%fused_computation.24 | convolution fusion | flops 17188257792 | bytes 29360128 | tf_op jit(solution)/shard_map/btk,kd->btd/dot_general | solution.py:85
  300.6 0.6 all-gather.16.cloned.1.call-update
  301.3 0.7 all-gather.18.cloned.1.call-update
  302.1 0.7 all-gather.20.cloned.1.call-update
  302.9 288.2 %all-reduce.3.cloned.1.call-done = bf16[1,2048,4096]{2,1,0:T(8,128)(2,1)} async-done(((bf16[1,2048,4096]{2,1,0:T(8,128)(2,1)}), bf16[1,2048,4096]{2,1,0:T(8,128)(2,1)}) %all-reduce.3.cloned.1.call-update) | async-done | bytes 16777232 | tf_op jit(solution)/shard_map/psum | solution.py:86
  591.1 20.1 %fusion.4 = (f32[2048]{0:T(1024)S(1)}, bf16[1,2048,4096]{2,1,0:T(8,128)(2,1)}) fusion(bf16[1,2048,4096]{2,1,0:T(8,128)(2,1)} %all-reduce.3.cloned.1.call-done, bf16[1,2048,4096]{2,1,0:T(8,128)(2,1)} %param.12), kind=kLoop, calls=%fused_computation.10 | loop fusion | flops 58718208 | bytes 50339840 | tf_op jit(solution)/shard_map/reduce_sum | solution.py:25
  611.2 117.4 %all-gather.16.cloned.1.call-done = bf16[4096,3584]{1,0:T(8,128)(2,1)} async-done(((bf16[512,3584]{1,0:T(8,128)(2,1)}), bf16[4096,3584]{1,0:T(8,128)(2,1)}) %all-gather.16.cloned.1.call-update) | async-done | bytes 29360144 | tf_op jit(solution)/shard_map/all_gather | solution.py:89
  728.6 72.0 %fusion.35 = f32[2048,3584]{1,0:T(8,128)} fusion(bf16[4096,3584]{1,0:T(8,128)(2,1)} %all-gather.16.cloned.1.call-done, bf16[1,2048,4096]{2,1,0:T(8,128)(2,1)} %get-tuple-element.7, f32[4096]{0:T(1024)S(1)} %convert_element_type.213, f32[2048]{0:T(1024)S(1)} %add_rsqrt_fusion), kind=kOutput, calls=%fused_computation.61 | convolution fusion | flops 60163096576 | bytes 75522048 | tf_op jit(solution)/shard_map/btd,df->btf/dot_general | solution.py:91
  800.7 66.7 %all-gather.18.cloned.1.call-done = bf16[4096,3584]{1,0:T(8,128)(2,1)} async-done(((bf16[512,3584]{1,0:T(8,128)(2,1)}), bf16[4096,3584]{1,0:T(8,128)(2,1)}) %all-gather.18.cloned.1.call-update) | async-done | bytes 29360144 | tf_op jit(solution)/shard_map/all_gather | solution.py:90
  867.4 78.3 %multiply_convert_fusion = bf16[2048,3584]{1,0:T(8,128)(2,1)} fusion(f32[2048,3584]{1,0:T(8,128)} %fusion.35, bf16[4096,3584]{1,0:T(8,128)(2,1)} %all-gather.18.cloned.1.call-done, bf16[1,2048,4096]{2,1,0:T(8,128)(2,1)} %get-tuple-element.7, f32[4096]{0:T(1024)S(1)} %convert_element_type.213, f32[2048]{0:T(1024)S(1)} %add_rsqrt_fusion), kind=kOutput, calls=%fused_computation.14 | convolution fusion | flops 60207136768 | bytes 90202112 | tf_op jit(solution)/shard_map/btd,df->btf/dot_general | solution.py:92
  945.7 60.4 %all-gather.20.cloned.1.call-done = bf16[3584,4096]{1,0:T(8,128)(2,1)} async-done(((bf16[3584,512]{1,0:T(8,128)(2,1)}), bf16[3584,4096]{1,0:T(8,128)(2,1)}) %all-gather.20.cloned.1.call-update) | async-done | bytes 29360144 | tf_op jit(solution)/shard_map/all_gather | solution.py:94
  1006.2 70.5 %convert_bitcast_fusion = bf16[1,2048,4096]{2,1,0:T(8,128)(2,1)} fusion(bf16[2048,3584]{1,0:T(8,128)(2,1)} %multiply_convert_fusion, bf16[3584,4096]{1,0:T(8,128)(2,1)} %all-gather.20.cloned.1.call-done), kind=kOutput, calls=%fused_computation.23 | convolution fusion | flops 60137930752 | bytes 60817408 | tf_op jit(solution)/shard_map/btf,fd->btd/dot_general | solution.py:95
  1076.8 1.2 copy-done.20
  1077.9 2.0 copy.36
  1080.0 2.0 copy.35
  1082.0 286.0 %all-reduce.5.cloned.1.call-done = bf16[1,2048,4096]{2,1,0:T(8,128)(2,1)} async-done(((bf16[1,2048,4096]{2,1,0:T(8,128)(2,1)}), bf16[1,2048,4096]{2,1,0:T(8,128)(2,1)}) %all-reduce.5.cloned.1.call-update) | async-done | bytes 16777232 | tf_op jit(solution)/shard_map/psum | solution.py:96
  1368.0 19.3 %fusion.7 = bf16[1,2048,4096]{2,1,0:T(8,128)(2,1)} fusion(bf16[1,2048,4096]{2,1,0:T(8,128)(2,1)} %get-tuple-element.7, bf16[1,2048,4096]{2,1,0:T(8,128)(2,1)} %all-reduce.5.cloned.1.call-done), kind=kLoop, calls=%fused_computation.13 | loop fusion | flops 33554432 | bytes 50331648 | tf_op jit(solution)/shard_map/convert_element_type | solution.py:97
  (114 shorter events, 1.5 us)
Async XLA Ops:
  7.2 27.6 %all-gather.10.cloned.1.call-start = ((), (), s32[]{:S(2)}) async-start(), calls=%async_computation.1 | async-start | bytes 2359296 | tf_op jit(solution)/shard_map/all_gather | solution.py:78
  8.0 51.5 %all-gather.8.cloned.1.call-start = ((), (), s32[]{:S(2)}) async-start(), calls=%async_computation | async-start | bytes 2359296 | tf_op jit(solution)/shard_map/all_gather | solution.py:79
  8.8 99.9 %all-gather.12.cloned.1.call-start = ((), (), s32[]{:S(2)}) async-start(), calls=%async_computation.2 | async-start | bytes 9437184 | tf_op jit(solution)/shard_map/all_gather | solution.py:77
  9.6 266.0 %all-gather.14.cloned.1.call-start = ((), (), s32[]{:S(2)}) async-start(), calls=%async_computation.3 | async-start | bytes 9437184 | tf_op jit(solution)/shard_map/all_gather | solution.py:84
  10.2 580.9 %all-reduce.3.cloned.1.call-start = ((), (), s32[]{:S(2)}) async-start(), calls=%async_computation.4 | async-start | bytes 33554432 | tf_op jit(solution)/shard_map/psum | solution.py:86
  10.4 7.3 copy-start.21
  10.4 7.3 copy-start.23
  21.8 210.6 %copy-start.8 = (pred[256,2048]{0,1:T(8,128)(4,1)}, pred[256,2048]{0,1:T(8,128)(4,1)S(1)}, u32[]{:S(2)}) copy-start(pred[256,2048]{0,1:T(8,128)(4,1)S(1)} %fusion.55) | copy-start | bytes 1572868
  22.5 190.9 %copy-start.10 = (pred[256,1536]{0,1:T(8,128)(4,1)}, pred[256,1536]{0,1:T(8,128)(4,1)S(1)}, u32[]{:S(2)}) copy-start(pred[256,1536]{0,1:T(8,128)(4,1)S(1)} %fusion.59) | copy-start | bytes 1179652
  22.8 166.9 %copy-start.12 = (pred[256,1280]{0,1:T(8,128)(4,1)}, pred[256,1280]{0,1:T(8,128)(4,1)S(1)}, u32[]{:S(2)}) copy-start(pred[256,1280]{0,1:T(8,128)(4,1)S(1)} %fusion.60) | copy-start | bytes 983044
  23.0 168.8 %copy-start.18 = (pred[256,1024]{0,1:T(8,128)(4,1)}, pred[256,1024]{0,1:T(8,128)(4,1)S(1)}, u32[]{:S(2)}) copy-start(pred[256,1024]{0,1:T(8,128)(4,1)S(1)} %fusion.131) | copy-start | bytes 786436
  38.8 9.0 copy-start.14
  38.8 9.0 copy-start.16
  48.2 155.8 %copy-start.2 = (bf16[1,2048,2,64]{1,3,2,0:T(8,128)(2,1)}, bf16[1,2048,2,64]{1,3,2,0:T(8,128)(2,1)S(1)}, u32[]{:S(2)}) copy-start(bf16[1,2048,2,64]{1,3,2,0:T(8,128)(2,1)S(1)} %get-tuple-element.10) | copy-start | bytes 1572868
  48.2 155.8 %copy-start.4 = (bf16[1,2048,2,64]{1,3,2,0:T(8,128)(2,1)}, bf16[1,2048,2,64]{1,3,2,0:T(8,128)(2,1)S(1)}, u32[]{:S(2)}) copy-start(bf16[1,2048,2,64]{1,3,2,0:T(8,128)(2,1)S(1)} %get-tuple-element.11) | copy-start | bytes 1572868
  120.6 23.9 %copy-start.15 = (f32[2048,64]{0,1:T(8,128)S(1)}, f32[2048,64]{0,1:T(8,128)}, u32[]{:S(2)}) copy-start(f32[2048,64]{0,1:T(8,128)} %get-tuple-element.12) | copy-start | bytes 1572868
  120.6 24.0 %copy-start.17 = (f32[2048,64]{0,1:T(8,128)S(1)}, f32[2048,64]{0,1:T(8,128)}, u32[]{:S(2)}) copy-start(f32[2048,64]{0,1:T(8,128)} %get-tuple-element.13) | copy-start | bytes 1572868
  157.7 8.2 copy-start
  157.7 8.2 copy-start.1
  174.7 14.9 %copy-start.6 = (f32[2,1280,256,4]{2,1,3,0:T(8,128)}, f32[2,1280,256,4]{2,1,3,0:T(8,128)S(1)}, u32[]{:S(2)}) copy-start(f32[2,1280,256,4]{2,1,3,0:T(8,128)S(1)} %get-tuple-element.23) | copy-start | bytes 31457284
  191.8 5.3 copy-start.7
  191.8 6.3 copy-start.9
  200.7 11.3 slice-start.11
  204.0 8.1 slice-start.12
  232.5 16.7 %slice-start.8 = ((s8[10485760]{0:T(1024)(128)(4,1)}), s8[2097152]{0:T(1024)(128)(4,1)S(1)}, s32[]{:S(2)}) async-start(s8[10485760]{0:T(1024)(128)(4,1)} %bitcast.476), calls=%async_computation.17 | async-start | bytes 4194304
  242.2 6.9 slice-start.9
  242.2 6.9 slice-start.10
  242.2 6.9 copy-start.13
  242.2 6.9 copy-start.19
  249.2 3.8 copy-start.11
  249.2 13.2 slice-start
  249.2 13.2 slice-start.1
  253.0 9.4 slice-start.2
  253.0 9.4 slice-start.3
  253.0 15.8 %slice-start.4 = ((s8[16777216]{0:T(1024)(128)(4,1)}), s8[4194304]{0:T(1024)(128)(4,1)S(1)}, s32[]{:S(2)}) async-start(s8[16777216]{0:T(1024)(128)(4,1)} %bitcast.472), calls=%async_computation.13 | async-start | bytes 8388608
  253.0 15.8 %slice-start.5 = ((s8[16777216]{0:T(1024)(128)(4,1)}), s8[4194304]{0:T(1024)(128)(4,1)S(1)}, s32[]{:S(2)}) async-start(s8[16777216]{0:T(1024)(128)(4,1)} %bitcast.472), calls=%async_computation.14 | async-start | bytes 8388608
  262.4 6.4 slice-start.6
  262.4 6.4 slice-start.7
  300.5 2.3 copy-start.22
  300.6 428.1 %all-gather.16.cloned.1.call-start = ((), (), s32[]{:S(2)}) async-start(), calls=%async_computation.5 | async-start | bytes 33030144 | tf_op jit(solution)/shard_map/all_gather | solution.py:89
  301.2 566.2 %all-gather.18.cloned.1.call-start = ((), (), s32[]{:S(2)}) async-start(), calls=%async_computation.6 | async-start | bytes 33030144 | tf_op jit(solution)/shard_map/all_gather | solution.py:90
  302.0 704.2 %all-gather.20.cloned.1.call-start = ((), (), s32[]{:S(2)}) async-start(), calls=%async_computation.7 | async-start | bytes 33030144 | tf_op jit(solution)/shard_map/all_gather | solution.py:94
  302.8 1065.2 %all-reduce.5.cloned.1.call-start = ((), (), s32[]{:S(2)}) async-start(), calls=%async_computation.8 | async-start | bytes 33554432 | tf_op jit(solution)/shard_map/psum | solution.py:96
  1076.7 1.2 copy-start.20
  1076.7 3.2 copy-start.3
  1076.7 3.2 copy-start.5
Sparse Core Ops, SparseCore 0:
  9.6 25.0 all-gather.9
  36.4 23.1 all-gather.7
  61.1 47.5 all-gather.11
  110.2 47.1 all-gather.13
  300.7 290.4 all-reduce.2
  592.6 136.0 all-gather.15
  730.2 137.1 all-gather.17
  869.0 137.1 all-gather.19
  1076.9 291.0 all-reduce.4
where the time goes:
time: 1400 us; the launch traced here: 1390 us
  waiting for transfers between devices  885 us (63%)
  matrix products  371 us (26%)
  other arithmetic  90.7 us (6%)
  local copies, waits for them, and re-layouts  30.8 us (2%)
  between operations  15.6 us (1%)
    psum x1, waiting for transfers between devices, local_layer(): y_attn = lax.psum(y_part, 'tp')  288 us
    psum x1, waiting for transfers between devices, local_layer(): down_val = lax.psum(down_part, 'tp')  286 us
    all_gather x1, waiting for transfers between devices, local_layer(): full_gate = lax.all_gather(w_gate, 'fsdp', axis=0, tiled=True)  117 us
    dot_general x1, matrix products, local_layer(): jnp.einsum('btd,df->btf', h_mlp, full_up, preferred_element_type=jnp.floa...  78.3 us
    dot_general x1, matrix products, local_layer(): jnp.einsum('btd,df->btf', h_mlp, full_gate, preferred_element_type=jnp.fl...  72 us
    dot_general x1, matrix products, local_layer(): jnp.einsum('btf,fd->btd', hidden_act, full_down, preferred_element_type=j...  70.5 us
    all_gather x1, waiting for transfers between devices, local_layer(): full_up = lax.all_gather(w_up, 'fsdp', axis=0, tiled=True)  66.7 us
    all_gather x1, waiting for transfers between devices, local_layer(): full_down = lax.all_gather(w_down, 'fsdp', axis=1, tiled=True)  60.4 us
  transfers between devices with their start and end apart: 9, of which 8 were waited for; matrix products, arithmetic and copies ran while one was open for 27% of the time, Pallas kernels for 0%

commit v1 on v0

v1 whole, which is shorter than its diff:
```python
import functools
import math
import jax
import jax.numpy as jnp
from jax import lax
from jax.experimental import pallas as pl
from jax.experimental.pallas import tpu as pltpu
from jax.sharding import PartitionSpec as P

HEAD_DIM = 128
ROPE_THETA = 500000.0
NORM_EPS = 1e-5
SCORE_SCALE = HEAD_DIM ** -0.5
LOG2E = 1.4426950408889634
BF16 = jnp.bfloat16
F32 = jnp.float32
N_REL = 4
N_ROWCH = 4
N_DOWN = 4
TILE = 256
GU_SPLIT = (0, 2, 6, 10, 14)
MESH = pl.DeviceIdType.MESH
VMEM_PLACE = 50331648


def rope_freqs():
    half_idx = jnp.arange(HEAD_DIM // 2, dtype=F32)
    inv_freq = jnp.power(ROPE_THETA, -2.0 * half_idx / HEAD_DIM)
    wave_len = 2.0 * math.pi / inv_freq
    smooth = (8192.0 / wave_len - 1.0) / 3.0
    blended = (1.0 - smooth) * inv_freq / 8.0 + smooth * inv_freq
    return jnp.where(wave_len < 2048.0, inv_freq, jnp.where(wave_len > 8192.0, inv_freq / 8.0, blended))


def layer_kernel(n_tp, n_fsdp, *refs):
    (pos_ref, len_ref, freq_ref, gains, tok, wk, wv, wq, wo, wg, wu, wd,
     kv_out, res, full_p, full_o, full_g, full_u, full_d, act, rs,
     u_buf, w_buf, p_buf, x1_buf, qkv_buf, o_buf, stage, r_buf, a_stage, cos_ref, sin_ref, bias_ref,
     x_send, x_recv, y_send, y_recv, w_sem, wd_sem, l_sem, b_sem, a_sem, r_sem, o_sem) = refs
    n_tok, width = tok.shape
    rows = n_tok // N_ROWCH
    sub = rows // N_REL
    k_rows = wk.shape[0]
    kv_cols = wk.shape[1]
    q_cols = wq.shape[1]
    ffn = wg.shape[1]
    o_cols = wo.shape[1]
    d_cols = wd.shape[1] // N_DOWN
    c_cols = d_cols * n_fsdp
    n_x = n_fsdp // 2

    me_t = lax.axis_index("tp")
    me_f = lax.axis_index("fsdp")
    chip, core = me_f // 2, me_f % 2
    t_right = lax.rem(me_t + 1, n_tp)
    t_left = lax.rem(me_t + n_tp - 1, n_tp)
    f_right = 2 * lax.rem(chip + 1, n_x) + core
    f_left = 2 * lax.rem(chip + n_x - 1, n_x) + core
    f_far = 2 * lax.rem(chip + 2, n_x) + core
    other = 1 - 2 * core
    f_twin = me_f + other

    barrier = pltpu.get_barrier_semaphore()
    for peer in ({"tp": t_left}, {"tp": t_right}, {"fsdp": f_left}, {"fsdp": f_right}, {"fsdp": f_twin}):
        pl.semaphore_signal(barrier, inc=1, device_id=peer, device_id_type=MESH)
    pl.semaphore_wait(barrier, 5)

    def al(val, mult):
        return pl.multiple_of(val, mult)

    pieces = []

    def add_piece(own, place):
        pieces.append((own, place, len(pieces) % 2))
        return len(pieces) - 1

    def by_rows(full, c0, c1):
        return lambda f: full.at[pl.ds(al(f * k_rows, k_rows), k_rows), pl.ds(c0, c1 - c0)]

    def halves(own, place):
        n = own.shape[0] // 2
        return tuple(add_piece(own.at[pl.ds(i * n, n), :], lambda f, i=i: place(f).at[pl.ds(i * n, n), :]) for i in range(2))

    def cols_of(own, full, c0, c1):
        return add_piece(own.at[:, pl.ds(c0, c1 - c0)], by_rows(full, c0, c1))

    half_q = q_cols // 2
    q_from = 2 * kv_cols
    pk = add_piece(wk, by_rows(full_p, 0, kv_cols))
    pv = add_piece(wv, by_rows(full_p, kv_cols, q_from))
    q0, q1 = [add_piece(wq.at[:, pl.ds(c, half_q)], by_rows(full_p, q_from + c, q_from + c + half_q)) for c in (0, half_q)]
    po = halves(wo, lambda f: full_o.at[:, pl.ds(al(f * o_cols, o_cols), o_cols)])
    pg = [tuple(cols_of(own, full, lo * TILE, hi * TILE) for own, full in ((wg, full_g), (wu, full_u)))
          for lo, hi in zip(GU_SPLIT, GU_SPLIT[1:])]
    pd = [halves(wd.at[:, pl.ds(k * d_cols, d_cols)], lambda f, k=k: full_d.at[k, :, pl.ds(al(f * d_cols, d_cols), d_cols)])
          for k in range(N_DOWN)]

    def x_copy(p, m):
        own, place, way = pieces[p]
        if m in (0, 1, 3):
            src, owner = own, me_f
        elif m == 2:
            owner = f_left if way == 0 else f_right
            src = place(owner)
        else:
            owner = {4: f_left, 5: f_right, 6: f_far}[m]
            src = place(owner)
        target = {0: f_right, 1: f_left, 2: f_right if way == 0 else f_left}.get(m, f_twin)
        return pltpu.make_async_remote_copy(src_ref=src, dst_ref=place(owner), send_sem=x_send.at[p, m], recv_sem=x_recv.at[p, m],
                                            device_id={"fsdp": target}, device_id_type=MESH)

    def x_wait(p, m):
        own, place, _ = pieces[p]
        owner = {0: f_left, 1: f_right, 2: f_far, 3: me_f + other, 4: f_left + other, 5: f_right + other, 6: f_far + other}[m]
        pltpu.make_async_remote_copy(src_ref=own, dst_ref=place(owner), send_sem=x_send.at[p, m], recv_sem=x_recv.at[p, m],
                                     device_id={"fsdp": f_twin}, device_id_type=MESH).wait_recv()

    def x_first(*ps):
        for p in ps:
            for m in (0, 1, 3):
                x_copy(p, m).start()

    def x_fwd(*ps):
        for p in ps:
            way = pieces[p][2]
            x_wait(p, way)
            x_copy(p, 2).start()
            x_copy(p, 4 + way).start()

    def x_side(*ps):
        for p in ps:
            way = 1 - pieces[p][2]
            x_wait(p, way)
            x_copy(p, 4 + way).start()

    def x_second(*ps):
        x_fwd(*ps)
        x_side(*ps)

    def x_third(*ps):
        for p in ps:
            x_wait(p, 2)
            x_copy(p, 6).start()

    def x_ready(*ps):
        for p in ps:
            for m in (3, 4, 5, 6):
                x_wait(p, m)

    unit_list = [(k, pair) for pair in range(2) for k in range(N_DOWN)]
    unit_at = [2 * k + pair for k, pair in unit_list]
    unit_order = {u: i for i, u in enumerate(unit_at)}

    def y_rows(e):
        if e < N_ROWCH:
            slot, lane, wid = e % 2, 0, width
        else:
            q = unit_order[e - N_ROWCH] % 4
            slot, lane, wid = q // 2, (q % 2) * (width // 2), 2 * c_cols
        return slot, lane, wid

    def lanes(e, h):
        slot, lane, wid = y_rows(e)
        return slot, pl.ds(lane + h * (wid // 2), wid // 2), pl.ds(h * (wid // 2), wid // 2)

    def g_slice(e, r):
        if e < N_ROWCH:
            return u_buf.at[pl.ds(e * rows + r * sub, sub), :]
        return res.at[e - N_ROWCH, r]

    FAR, NEAR, SUM, RIGHT, LEFT, PASS = range(6)

    def y_copy(e, m, h=0):
        slot, here, there = lanes(e, h)
        if m in (RIGHT, LEFT):
            src, dst, to = g_slice(e, 0), g_slice(e, m - 2), m - 3
            if e >= N_ROWCH:
                src, dst = r_buf.at[unit_order[e - N_ROWCH] % 2, :, there], dst.at[:, there]
        elif m == PASS:
            src, dst, to = g_slice(e, 2 - h).at[:, there], g_slice(e, 3).at[:, there], 1 - h
        else:
            r, i, to = {FAR: (3, 0, h), NEAR: (1 + h, 2 - h, 1 - h), SUM: (2 - h, 1 + h, h)}[m]
            src, dst = p_buf.at[slot, pl.ds(r * sub, sub), here], rs.at[e, i, :, there]
        return pltpu.make_async_remote_copy(src_ref=src, dst_ref=dst, send_sem=y_send.at[e, m, h], recv_sem=y_recv.at[e, m, h],
                                            device_id={"tp": t_right if to == 0 else t_left}, device_id_type=MESH)

    def rs_slice(e, i):
        return rs.at[e, i, :, pl.ds(0, y_rows(e)[2])]

    def load_stage(e, idx):
        wid = y_rows(e)[2]
        for i in idx:
            pltpu.make_async_copy(rs_slice(e, i), stage.at[i, :, pl.ds(0, wid)], l_sem.at[i]).start()

    def wait_stage(e, idx):
        wid = y_rows(e)[2]
        for i in idx:
            pltpu.make_async_copy(rs_slice(e, i), stage.at[i, :, pl.ds(0, wid)], l_sem.at[i]).wait()

    def y_start(e, hs=(0, 1)):
        for m in (FAR, NEAR):
            for h in hs:
                y_copy(e, m, h).start()

    def y_have(e, hs=(0, 1)):
        for h in hs:
            y_copy(e, NEAR, h).wait_recv()
            y_copy(e, SUM, h).wait_recv()

    def y_send_all(e, hs=(0,)):
        for h in hs:
            y_copy(e, LEFT, h).start()
            y_copy(e, RIGHT, h).start()

    def y_sent_all(e, hs=(0,)):
        for h in hs:
            y_copy(e, LEFT, h).wait_send()
            y_copy(e, RIGHT, h).wait_send()

    EW = 32

    def y_add(e):
        for h in (0, 1):
            slot, here, there = lanes(e, h)
            y_copy(e, FAR, h).wait_recv()
            pltpu.make_async_copy(rs.at[e, 0, :, there], stage.at[0, :, there], l_sem.at[h]).start()
        for h in (0, 1):
            slot, here, there = lanes(e, h)
            pltpu.make_async_copy(rs.at[e, 0, :, there], stage.at[0, :, there], l_sem.at[h]).wait()

            def body(i, carry, h=h, here=here, there=there):
                rr = pl.ds(al((2 - h) * sub + i * EW, EW), EW)
                tot = p_buf[slot, rr, here].astype(F32) + stage[0, pl.ds(al(i * EW, EW), EW), there].astype(F32)
                p_buf[slot, rr, here] = tot.astype(BF16)
                return carry

            lax.fori_loop(0, sub // EW, body, 0)
            y_copy(e, SUM, h).start()

    def tok_copy(c):
        row0 = al(c * rows + me_t * sub, sub)
        return pltpu.make_async_copy(tok.at[pl.ds(row0, sub), :], stage.at[0], l_sem.at[3])

    def y_norm(c):
        slot = c % 2
        tok_copy(c).start()
        y_have(c)
        load_stage(c, (1, 2))
        wait_stage(c, (1, 2))
        tok_copy(c).wait()

        def body(i, carry):
            rr = al(i * EW, EW)
            here = pl.ds(rr, EW)
            tot = p_buf[slot, here, :].astype(F32) + stage[1, here, :].astype(F32) + stage[2, here, :].astype(F32)
            x1 = (stage[0, here, :].astype(F32) + tot).astype(BF16)
            x1_buf[pl.ds(al(c * sub + i * EW, EW), EW), :] = x1
            xf = x1.astype(F32)
            inv = lax.rsqrt(jnp.mean(xf * xf, axis=-1, keepdims=True) + NORM_EPS)
            u_buf[pl.ds(al(c * rows + i * EW, EW), EW), :] = (xf * inv * gains[1:, :]).astype(BF16)
            return carry

        lax.fori_loop(0, sub // EW, body, 0)
        y_send_all(c)

    def y_final(k, pair):
        unit = 2 * k + pair
        e = N_ROWCH + unit
        r_slot = unit_order[unit] % 2
        if unit_order[unit] >= 2:
            before = N_ROWCH + unit_at[unit_order[unit] - 2]
            y_sent_all(before, (0, 1))
            r_out(before).wait()
        for h in (0, 1):
            slot, mine, there = lanes(e, h)
            y_have(e, (h,))
            loads = [pltpu.make_async_copy(rs.at[e, i, :, there], stage.at[i, :, there], l_sem.at[i]) for i in (1, 2)]
            for cp in loads:
                cp.start()
            for cp in loads:
                cp.wait()

            def body(i, carry, h=h, slot=slot, mine=mine):
                here = pl.ds(al(i * EW, EW), EW)
                x_rows = pl.ds(al((2 * pair + h) * sub + i * EW, EW), EW)
                for f in range(n_fsdp):
                    at = pl.ds(h * c_cols + f * d_cols, d_cols)
                    tot = (p_buf[slot, here, pl.ds(mine.start + f * d_cols, d_cols)].astype(F32)
                           + stage[1, here, at].astype(F32) + stage[2, here, at].astype(F32))
                    x1 = x1_buf[x_rows, pl.ds((f * N_DOWN + k) * d_cols, d_cols)].astype(F32)
                    r_buf[r_slot, here, at] = (x1 + tot).astype(BF16)
                return carry

            lax.fori_loop(0, sub // EW, body, 0)
            y_send_all(e, (h,))
        r_out(e).start()

    def r_out(e):
        return pltpu.make_async_copy(r_buf.at[unit_order[e - N_ROWCH] % 2], res.at[e - N_ROWCH, 0], r_sem.at[unit_order[e - N_ROWCH] % 2])

    def y_pass(e):
        for h in (0, 1):
            y_copy(e, LEFT - h, h if e >= N_ROWCH else 0).wait_recv()
            y_copy(e, PASS, h).start()

    def y_ready(e):
        for h in (0, 1):
            if e >= N_ROWCH:
                y_copy(e, RIGHT + h, h).wait_recv()
            y_copy(e, PASS, h).wait_recv()

    def bounce(src, via, dst, i):
        return pltpu.make_async_copy(src, via, b_sem.at[0, i]), pltpu.make_async_copy(via, dst, b_sem.at[1, i])

    small = [
        bounce(wk, w_buf.at[0, pl.ds(0, k_rows), pl.ds(0, kv_cols)], pieces[pk][1](me_f), 0),
        bounce(wv, w_buf.at[0, pl.ds(0, k_rows), pl.ds(kv_cols, kv_cols)], pieces[pv][1](me_f), 1),
        bounce(wq.at[:, pl.ds(0, half_q)], w_buf.at[0, pl.ds(k_rows, k_rows), :], pieces[q0][1](me_f), 2),
        bounce(wq.at[:, pl.ds(half_q, half_q)], w_buf.at[0, pl.ds(2 * k_rows, k_rows), :], pieces[q1][1](me_f), 3),
        bounce(wo, w_buf.at[0, pl.ds(3 * k_rows, wo.shape[0]), :], full_o.at[:, pl.ds(al(me_f * o_cols, o_cols), o_cols)], 4),
    ] + [
        bounce(wd.at[:, pl.ds(k * d_cols, d_cols)], w_buf.at[1, pl.ds(0, ffn), pl.ds(k * d_cols, d_cols)], full_d.at[k, :, pl.ds(al(me_f * d_cols, d_cols), d_cols)], 5 + k)
        for k in range(N_DOWN)
    ]
    large = [
        bounce(wg, p_buf.at[0, :, pl.ds(0, ffn)], full_g.at[pl.ds(al(me_f * k_rows, k_rows), k_rows), :], 9),
        bounce(wu, p_buf.at[1, :, pl.ds(0, ffn)], full_u.at[pl.ds(al(me_f * k_rows, k_rows), k_rows), :], 10),
    ]

    def bounce_in(group):
        for a, _ in group:
            a.start()

    def bounce_out(group):
        for a, b in group:
            a.wait()
            b.start()

    def bounce_end(group):
        for _, b in group:
            b.wait()

    def norm_rows(late):
        n_tile = n_tok // rows

        def load(i):
            return pltpu.make_async_copy(tok.at[pl.ds(i * rows, rows), :], p_buf.at[i % 2], w_sem.at[i % 2])

        load(0).start()
        for i in range(n_tile):
            if i + 1 < n_tile:
                load(i + 1).start()
            load(i).wait()

            def body(j, carry, i=i):
                vals = p_buf[i % 2, pl.ds(al(j * EW, EW), EW), :].astype(F32)
                inv = lax.rsqrt(jnp.mean(vals * vals, axis=-1, keepdims=True) + NORM_EPS)
                u_buf[pl.ds(al(i * rows + j * EW, EW), EW), :] = (vals * inv * gains[:1, :]).astype(BF16)
                return carry

            lax.fori_loop(0, rows // EW, body, 0)
            if i == n_tile - 2:
                late()

    def tables():
        sign = jnp.where(lax.broadcasted_iota(jnp.int32, (1, HEAD_DIM), 1) < HEAD_DIM // 2, -1.0, 1.0)
        first = pos_ref[0, 0]

        def body(i, carry):
            here = pl.ds(al(i * sub, sub), sub)
            row = first + i * sub + lax.broadcasted_iota(jnp.int32, (sub, HEAD_DIM), 0)
            angle = row.astype(F32) * freq_ref[...]
            cos_ref[here, :] = jnp.cos(angle)
            sin_ref[here, :] = sign * jnp.sin(angle)
            return carry

        lax.fori_loop(0, n_tok // sub, body, 0)
        key = lax.broadcasted_iota(jnp.int32, (1, n_tok), 1)
        bias_ref[...] = jnp.where(key < len_ref[0], 0.0, -jnp.inf)

    def stream(n0, n1, load, compute, hooks={}, lazy=()):
        def fetch(n, slot):
            for cp in load(n, slot):
                cp.start()

        fetch(n0, 0)

        def body(n, carry):
            slot = lax.rem(n - n0, 2)
            late = functools.reduce(jnp.logical_or, [n + 1 == at for at in lazy], n + 1 >= n1)
            pl.when(jnp.logical_not(late))(lambda: fetch(n + 1, 1 - slot))
            for cp in load(n, slot):
                cp.wait()
            compute(n, slot)
            for at, todo in hooks.items():
                @pl.when(n == at)
                def _(at=at, todo=todo):
                    todo()
                    if at + 1 in lazy:
                        fetch(at + 1, 1 - slot)
            return carry

        lax.fori_loop(n0, n1, body, 0)

    def project(hooks, lazy):
        def load(n, slot):
            return (pltpu.make_async_copy(full_p.at[:, pl.ds(al(n * TILE, TILE), TILE)], w_buf.at[slot, :, pl.ds(0, TILE)], w_sem.at[slot]),)

        def compute(n, slot):
            plain = n == 1

            def body(m, carry):
                here = pl.ds(al(m * 2 * rows, rows), 2 * rows)
                acc = jnp.dot(u_buf[here, :], w_buf[slot, :, :TILE], preferred_element_type=F32)
                cos_t = jnp.where(plain, 1.0, cos_ref[here, :])
                sin_t = jnp.where(plain, 0.0, sin_ref[here, :])
                for h in range(TILE // HEAD_DIM):
                    val = acc[:, h * HEAD_DIM:(h + 1) * HEAD_DIM]
                    val = val * cos_t + pltpu.roll(val, HEAD_DIM // 2, 1) * sin_t
                    qkv_buf[here, pl.ds(al(n * TILE + h * HEAD_DIM, HEAD_DIM), HEAD_DIM)] = val.astype(BF16)
                return carry

            lax.fori_loop(0, n_tok // (2 * rows), body, 0)

        stream(0, full_p.shape[1] // TILE, load, compute, hooks, lazy)

    def attend(c, mid=None):
        blk = 2 * sub
        n_blk = rows // blk
        n_old = c * rows
        n_head = q_cols // HEAD_DIM
        per_grp = q_cols // kv_cols
        dims = (((1,), (1,)), ((), ()))
        here = pl.ds(n_old, rows)

        def body(idx, carry):
            head = idx // n_blk
            part = lax.rem(idx, n_blk)
            row0 = al(part * blk, blk)
            col0 = al(head * HEAD_DIM, HEAD_DIM)
            k_at = al((head // per_grp) * HEAD_DIM, HEAD_DIM)
            k_cols, v_cols = pl.ds(k_at, HEAD_DIM), pl.ds(al(kv_cols + k_at, HEAD_DIM), HEAD_DIM)
            q_blk = qkv_buf[pl.ds(al(n_old + row0, blk), blk), pl.ds(al(q_from + col0, HEAD_DIM), HEAD_DIM)]
            s_new = lax.dot_general(q_blk, qkv_buf[here, k_cols], dims, preferred_element_type=F32)
            s_new = s_new * (SCORE_SCALE * LOG2E) + bias_ref[:, here]
            q_idx = row0 + lax.broadcasted_iota(jnp.int32, (blk, rows), 0)
            k_idx = lax.broadcasted_iota(jnp.int32, (blk, rows), 1)
            s_new = jnp.where(k_idx <= q_idx, s_new, -jnp.inf)
            top = jnp.max(s_new, axis=1, keepdims=True)
            if n_old:
                s_old = lax.dot_general(q_blk, qkv_buf[:n_old, k_cols], dims, preferred_element_type=F32)
                s_old = s_old * (SCORE_SCALE * LOG2E) + bias_ref[:, :n_old]
                top = jnp.maximum(top, jnp.max(s_old, axis=1, keepdims=True))
            p_new = jnp.exp2(s_new - top)
            den = jnp.sum(p_new, axis=1, keepdims=True)
            acc = jnp.dot(p_new.astype(BF16), qkv_buf[here, v_cols], preferred_element_type=F32)
            if n_old:
                p_old = jnp.exp2(s_old - top)
                den = den + jnp.sum(p_old, axis=1, keepdims=True)
                acc = acc + jnp.dot(p_old.astype(BF16), qkv_buf[:n_old, v_cols], preferred_element_type=F32)
            out = (acc / den).astype(BF16)
            for s in range(blk // sub):
                dist = lax.rem(part * (blk // sub) + s - me_t + n_tp, n_tp)
                pos = jnp.where(dist == 0, 0, jnp.where(dist == n_tp - 1, 1, dist + 1))
                o_buf[c % 2, pl.ds(al(pos * sub, sub), sub), pl.ds(col0, HEAD_DIM)] = out[s * sub:(s + 1) * sub, :]
            if mid:
                pl.when(idx == n_head)(mid)
            return carry

        lax.fori_loop(0, n_head * n_blk, body, 0)

    def o_place(n):
        depth = wo.shape[0]
        per = width // depth
        return n // per, pl.ds(al(lax.rem(n, per) * depth, depth), depth)

    def o_tile(n):
        slot, here = o_place(n)
        return pltpu.make_async_copy(full_o.at[:, pl.ds(al(n * o_cols, o_cols), o_cols)], w_buf.at[slot, here, :], o_sem.at[n])

    def out_load():
        def body(n, carry):
            o_tile(n).start()
            return carry

        lax.fori_loop(0, n_fsdp, body, 0)

    def out_project(c):
        def body(n, carry):
            if c == 0:
                o_tile(n).wait()
            slot, here = o_place(n)
            acc = jnp.dot(o_buf[c % 2], w_buf[slot, here, :], preferred_element_type=F32)
            p_buf[c % 2, :, pl.ds(al(n * o_cols, o_cols), o_cols)] = acc.astype(BF16)
            return carry

        lax.fori_loop(0, n_fsdp, body, 0)

    def act_copy(c0, nc, n, slot):
        return pltpu.make_async_copy(a_stage.at[slot, pl.ds(0, nc * rows), :],
                                     act.at[pl.ds(c0 * rows, nc * rows), pl.ds(al(n * TILE, TILE), TILE)], a_sem.at[slot])

    def gate_up(pair, n0, n1, hooks={}):
        c0, nc = 2 * pair, 2
        def load(n, slot):
            here = pl.ds(al(n * TILE, TILE), TILE)
            return (pltpu.make_async_copy(full_g.at[:, here], w_buf.at[slot, :, pl.ds(0, TILE)], w_sem.at[slot]),
                    pltpu.make_async_copy(full_u.at[:, here], w_buf.at[slot, :, pl.ds(TILE, TILE)], w_sem.at[2 + slot]))

        def compute(n, slot):
            lhs = u_buf[c0 * rows:(c0 + nc) * rows, :]
            gate = jnp.dot(lhs, w_buf[slot, :, :TILE], preferred_element_type=F32)
            gate = gate * jax.nn.sigmoid(gate)
            val = gate * jnp.dot(lhs, w_buf[slot, :, TILE:], preferred_element_type=F32)

            @pl.when(n - n0 >= 2)
            def _():
                act_copy(c0, nc, n, slot).wait()
            a_stage[slot, :nc * rows, :] = val.astype(BF16)
            act_copy(c0, nc, n, slot).start()

        stream(n0, n1, load, compute, hooks)
        for i in range(min(2, n1 - n0)):
            act_copy(c0, nc, n1 - 1, (n1 - 1 - i - n0) % 2).wait()

    def load_act(pair, start=True):
        c0, nc = 2 * pair, 2
        cp = pltpu.make_async_copy(act.at[pl.ds(c0 * rows, nc * rows), :], u_buf.at[pl.ds(c0 * rows, nc * rows), pl.ds(0, ffn)], l_sem.at[4])
        cp.start() if start else cp.wait()

    def down(k, pair, cs):
        e = N_ROWCH + 2 * k + pair
        slot_p, lane, _ = y_rows(e)
        half = ffn // 2
        row0, n_row = (2 * pair + cs[0]) * rows, len(cs) * rows

        def place(slot, i):
            return pl.ds(0, half), pl.ds(al((2 * slot + i) * TILE, TILE), TILE)

        def load(n, slot):
            return [pltpu.make_async_copy(full_d.at[k, pl.ds(i * half, half), pl.ds(al(n * TILE, TILE), TILE)],
                                          qkv_buf.at[place(slot, i)], wd_sem.at[2 * slot + i]) for i in range(2)]

        def compute(n, slot):
            prod = sum(jnp.dot(u_buf[row0:row0 + n_row, i * half:(i + 1) * half], qkv_buf[place(slot, i)], preferred_element_type=F32)
                       for i in range(2)).astype(BF16)
            for i, ci in enumerate(cs):
                p_buf[slot_p, :, pl.ds(al(lane + ci * c_cols + n * TILE, TILE), TILE)] = prod[i * rows:(i + 1) * rows, :]

        stream(0, c_cols // TILE, load, compute)

    def sent(e):
        for m in (FAR, NEAR, SUM):
            for h in (0, 1):
                y_copy(e, m, h).wait_send()

    def passed(e):
        for h in (0, 1):
            y_copy(e, PASS, h).wait_send()

    def scoped(fn):
        def run(*args, **kw):
            with jax.named_scope("_".join([fn.__name__] + [str(a) for a in args if isinstance(a, int)])):
                return fn(*args, **kw)
        return run

    x_first, x_fwd, x_side, x_third, x_ready = map(scoped, (x_first, x_fwd, x_side, x_third, x_ready))
    y_start, y_add, y_norm, y_final, y_pass, y_ready = map(scoped, (y_start, y_add, y_norm, y_final, y_pass, y_ready))
    norm_rows, project, attend, out_project, gate_up, down = map(scoped, (norm_rows, project, attend, out_project, gate_up, down))
    tables, bounce_in, bounce_out, bounce_end, sent, load_act = map(scoped, (tables, bounce_in, bounce_out, bounce_end, sent, load_act))

    def x_done(*ps):
        x_third(*ps)
        x_ready(*ps)

    def sent_u(*cs):
        for c in cs:
            y_sent_all(c)
            passed(c)

    c0, c1, c2, c3 = range(N_ROWCH)
    units = [N_ROWCH + u for u in unit_at]
    g0, g1, g2, g3 = pg
    d0, d1, d2, d3 = pd
    t0, t1, t2, t3, t4 = GU_SPLIT

    def begin(i):
        if i >= 4:
            sent(units[i - 4])
        parts = ((0,), (1,)) if i == 0 else ((0, 1),)
        for cs in parts:
            down(*unit_list[i], cs)
            y_start(units[i], cs)

    x_first(pk, pv, q0)
    bounce_in(small)
    norm_rows(lambda: x_second(pk, pv))
    bounce_out(small)
    bounce_in(large)
    tables()
    x_fwd(q0)
    x_first(q1)
    x_done(pk, pv)
    bounce_end(small)
    kv_copy = pltpu.make_async_copy(qkv_buf.at[:, pl.ds(0, q_from)], kv_out, r_sem.at[2])

    def have_kv():
        bounce_out(large)
        kv_copy.start()
        x_side(q0)
        x_done(q0)

    project({
        0: lambda: (x_fwd(q1), x_first(*po)),
        1: have_kv,
        3: lambda: (x_side(q1), x_done(q1)),
        4: lambda: (x_second(*po), x_first(*g0, *g1, *g2)),
    }, (2, 4))
    attend(c0)
    x_done(*po)
    out_load()
    bounce_end(large)
    out_project(c0)
    y_start(c0)
    attend(c1)
    out_project(c1)
    y_start(c1)
    x_second(*g0)
    attend(c2, lambda: y_add(c0))
    attend(c3, lambda: y_add(c1))
    x_second(*g1)
    y_norm(c0)
    y_norm(c1)
    sent(c0)
    out_project(c2)
    sent(c1)
    out_project(c3)
    y_pass(c0)
    y_pass(c1)
    y_start(c2)
    y_start(c3)
    x_second(*g2)
    x_first(*g3)
    x_third(*g0)
    x_third(*g1)
    x_ready(*g0)
    y_ready(c0)
    y_ready(c1)
    x_ready(*g1)
    gate_up(0, t0, t3, {t1: lambda: (x_third(*g2), y_add(c2)), t2 - 2: lambda: x_ready(*g2), t2 + 1: lambda: y_add(c3)})
    x_second(*g3)
    x_first(*d0)
    y_norm(c2)
    y_norm(c3)
    x_done(*g3)
    y_pass(c2)
    gate_up(0, t3, t4, {t3 + 1: lambda: (x_second(*d0), x_first(*d1)), t4 - 2: lambda: y_pass(c3)})
    sent_u(c0, c1)
    load_act(0)
    x_done(*d0)
    load_act(0, False)
    kv_copy.wait()
    sent(c2)
    sent(c3)
    begin(0)
    x_second(*d1)
    x_first(*d2)
    y_ready(c2)
    y_ready(c3)
    sent_u(c2, c3)
    f0, f1, f2, f3 = units[:N_DOWN]
    gate_up(1, t0, t4, {
        1: lambda: (y_add(f0), x_done(*d1), begin(1)),
        2: lambda: y_final(*unit_list[0]),
        3: lambda: (x_second(*d2), x_first(*d3)),
        4: lambda: y_add(f1),
        5: lambda: (y_pass(f0), x_third(*d2)),
        6: lambda: (y_final(*unit_list[1]), x_ready(*d2), begin(2)),
        7: lambda: x_second(*d3),
        8: lambda: y_pass(f1),
        9: lambda: (y_add(f2), x_done(*d3), begin(3)),
        10: lambda: y_final(*unit_list[2]),
        12: lambda: y_add(f3),
    })
    load_act(1)
    y_pass(f2)
    load_act(1, False)
    n_unit = len(units)
    half = n_unit // 2
    begin(half)
    y_final(*unit_list[half - 1])
    for i in range(half, n_unit):
        if i + 1 < n_unit:
            begin(i + 1)
        y_add(units[i])
        y_pass(units[i - 1])
        y_final(*unit_list[i])
    y_pass(units[-1])

    for e in units:
        y_ready(e)
        passed(e)
    for e in units[-4:]:
        sent(e)
    for e in units[-2:]:
        y_sent_all(e, (0, 1))
        r_out(e).wait()
    for p in range(len(pieces)):
        for m in range(7):
            x_copy(p, m).wait_send()


def place_kernel(n_tp, n_fsdp, *refs):
    srcs, out_ref = refs[:N_DOWN], refs[N_DOWN]
    sub = srcs[0].shape[2]
    cols = srcs[0].shape[3] // n_fsdp
    for r, dist in enumerate((0, n_tp - 1, 1, 2)):
        here = pl.ds(pl.multiple_of(lax.rem(lax.axis_index("tp") + dist, n_tp) * sub, sub), sub)
        for k in range(N_DOWN):
            for f in range(n_fsdp):
                c0 = (f * N_DOWN + k) * cols
                out_ref[here, c0:c0 + cols] = srcs[k][0, r, :, f * cols:(f + 1) * cols]


def place(res, n_tok, width, n_tp, n_fsdp):
    sub, c_cols = res.shape[2], res.shape[3] // 2

    def src_spec(k):
        return pl.BlockSpec((1, N_REL, sub, c_cols), lambda c: (2 * k + c // 2, 0, 0, c % 2))

    return pl.pallas_call(
        functools.partial(place_kernel, n_tp, n_fsdp),
        out_shape=jax.ShapeDtypeStruct((n_tok, width), BF16),
        grid=(N_ROWCH,),
        in_specs=[src_spec(k) for k in range(N_DOWN)],
        out_specs=pl.BlockSpec((N_REL * sub, width), lambda c: (c, 0)),
        compiler_params=pltpu.CompilerParams(vmem_limit_bytes=VMEM_PLACE),
        name="place",
    )(*([res] * N_DOWN))


def solution(mesh):
    batch_axes = ('dp', 'fsdp')
    n_tp = mesh.shape['tp']
    n_fsdp = mesh.shape['fsdp']
    in_specs = (P(batch_axes, None, None), P(batch_axes, None), P(batch_axes),
                P('fsdp', 'tp'), P('fsdp', 'tp'), P('fsdp', 'tp'), P('tp', 'fsdp'),
                P('fsdp', 'tp'), P('fsdp', 'tp'), P('tp', 'fsdp'), P(None), P(None))
    out_specs = (P(batch_axes, None, None), P(batch_axes, None, 'tp', None), P(batch_axes, None, 'tp', None))

    def local_layer(tokens, positions, valid_len, w_query, w_key, w_value, w_out, w_gate, w_up, w_down, norm_attn, norm_mlp):
        n_tok, width = tokens.shape[1], tokens.shape[2]
        ffn = w_gate.shape[1]
        rows, sub = n_tok // N_ROWCH, n_tok // N_ROWCH // N_REL
        q_cols, kv_cols = w_query.shape[1], w_key.shape[1]
        c_cols = width // N_DOWN
        n_units = 2 * N_DOWN
        freqs = jnp.tile(rope_freqs(), 2)[None]
        gains = jnp.stack([norm_attn, norm_mlp]).astype(F32)
        vm = pl.BlockSpec(memory_space=pltpu.VMEM)
        smem = pl.BlockSpec(memory_space=pltpu.SMEM)
        hbm = pl.BlockSpec(memory_space=pl.ANY)
        n_pieces = 6 + 2 * (len(GU_SPLIT) - 1 + N_DOWN)
        n_y = N_ROWCH + n_units
        st = lambda *s: jax.ShapeDtypeStruct(s, BF16)
        dma = pltpu.SemaphoreType.DMA
        outs = pl.pallas_call(
            functools.partial(layer_kernel, n_tp, n_fsdp),
            out_shape=[st(n_tok, 2 * kv_cols), st(n_units, N_REL, sub, 2 * c_cols),
                       st(width, 2 * kv_cols + q_cols), st(w_out.shape[0], width),
                       st(width, ffn), st(width, ffn), st(N_DOWN, ffn, c_cols), st(n_tok, ffn), st(n_y, 3, sub, width)],
            in_specs=[smem] * 2 + [vm] * 2 + [hbm] * 8,
            out_specs=[hbm] * 9,
            scratch_shapes=[
                pltpu.VMEM((n_tok, width), BF16), pltpu.VMEM((2, width, 2 * TILE), BF16),
                pltpu.VMEM((2, rows, width), BF16),
                pltpu.VMEM((rows, width), BF16), pltpu.VMEM((n_tok, 2 * kv_cols + q_cols), BF16),
                pltpu.VMEM((2, rows, q_cols), BF16), pltpu.VMEM((3, sub, width), BF16),
                pltpu.VMEM((2, sub, 2 * c_cols), BF16), pltpu.VMEM((2, 2 * rows, TILE), BF16),
                pltpu.VMEM((n_tok, HEAD_DIM), F32), pltpu.VMEM((n_tok, HEAD_DIM), F32), pltpu.VMEM((1, n_tok), F32),
                dma((n_pieces, 7)), dma((n_pieces, 7)), dma((n_y, 6, 2)), dma((n_y, 6, 2)),
                dma((4,)), dma((4,)), dma((5,)), dma((2, 11)), dma((2,)), dma((3,)), dma((n_fsdp,)),
            ],
            compiler_params=pltpu.CompilerParams(vmem_limit_bytes=67043328, collective_id=0, has_side_effects=True),
            name="layer",
        )(positions, valid_len, freqs, gains, tokens[0],
          w_key, w_value, w_query, w_out, w_gate, w_up, w_down)
        kv_all, res = outs[0], outs[1]
        hidden = place(res, n_tok, width, n_tp, n_fsdp)
        n_kv = kv_cols // HEAD_DIM
        key_cache = kv_all[:, :kv_cols].reshape(1, n_tok, n_kv, HEAD_DIM)
        value_cache = kv_all[:, kv_cols:].reshape(1, n_tok, n_kv, HEAD_DIM)
        return hidden[None], key_cache, value_cache

    return jax.shard_map(local_layer, mesh=mesh, in_specs=in_specs, out_specs=out_specs, check_vma=False)
```

time: 1400 us -> 691 us (0.49)
  waiting for transfers between devices: 885 us -> 0 us
  Pallas kernels: 0 us -> 682 us
  matrix products: 371 us -> 0 us
  other arithmetic: 90.7 us -> 0.68 us
  local copies, waits for them, and re-layouts: 30.8 us -> 4.36 us
  between operations: 15.6 us -> 1.31 us
    pallas_call x0 -> x2, Pallas kernels: none -> 682 us  [the longest x1 670 us: local_layer(): pl.pallas_call(functools.partial(layer_kernel, n_tp, n_fsdp), out_shape=[...]
    psum x2 -> x0, waiting for transfers between devices: 574 us -> none  [the longest x1 288 us: local_layer(): y_attn = lax.psum(y_part, 'tp')]
    dot_general x23 -> x0, matrix products: 371 us -> none  [the longest x1 78.3 us: local_layer(): jnp.einsum('btd,df->btf', h_mlp, full_up, preferred_element_type=jnp.floa...]
    all_gather x7 -> x0, waiting for transfers between devices: 306 us -> none  [the longest x1 117 us: local_layer(): full_gate = lax.all_gather(w_gate, 'fsdp', axis=0, tiled=True)]
    reduce_sum x10 -> x0, other arithmetic: 62.5 us -> none  [the longest x8 35.2 us: attention(): attn_prob = jax.nn.softmax(scores, axis=-1).astype(jnp.bfloat16)]
    convert_element_type x4 -> x1, other arithmetic: 19.3 us -> 0.66 us  [local_layer(): gains = jnp.stack([norm_attn, norm_mlp]).astype(F32)]
    dot_general x2 -> x0, local copies, waits for them, and re-layouts: 16 us -> none  [the longest x1 11.9 us: local_layer(): jnp.einsum('btd,dk->btk', h_in, full_q, preferred_element_type=jnp.float32)]
  transfers between devices with their start and end apart: 9 -> 0, of which waited for: 8 -> 0; matrix products, arithmetic and copies ran while one was open for 27% -> 0% of each run, Pallas kernels for 0% -> 0%
where the time goes in v1:
time: 691 us; the launch traced here: 689 us
  Pallas kernels  682 us (99%)
    pallas_call x1, Pallas kernels, local_layer(): pl.pallas_call(functools.partial(layer_kernel, n_tp, n_fsdp), out_shape=[...  670 us

profile of v1, /device:TPU:96, one launch (start us, length us, event | category | flops | bytes accessed | tf_op | source)
XLA Modules:
  0.0 688.7 jit_solution(3336271007821358655)
XLA Ops:
  1.3 0.6 broadcast_in_dim_tile.3.refs_2_
  1.9 0.7 stack.9
  2.6 0.7 stack.10
  3.3 0.7 maximum_convert_fusion.refs_3_
  4.0 669.9 %layer.1 = (bf16[2048,512]{1,0:T(8,128)(2,1)}, bf16[8,4,128,2048]{3,2,1,0:T(8,128)(2,1)}, bf16[4096,1536]{1,0:T(8,128)(2,1)}, bf16[1024,4096]{1,0:T(8,128)(2,1)}...) custom-call(s32[1,2048]{1,0:T(1,128)} %refs_0_.1, ...), custom_call_target="tpu_custom_call" | custom-call | tf_op jit(solution)/shard_map/layer/pallas_call | solution.py:767
  673.9 0.0 copy-start
  673.9 12.5 %place.1 = bf16[2048,4096]{1,0:T(8,128)(2,1)} custom-call(bf16[8,4,128,2048]{3,2,1,0:T(8,128)(2,1)} %get-tuple-element.5.refs_0_.refs_1_.refs_2_.refs_3_, bf16[8,4,128,2048]{3,2,1,0:T(8,128)(2,1)} %get-tuple-element.5.refs_0_.refs_1_.refs_2_.refs_3_, bf16[8,4,128,2048]{3,2,1,0:T(8,128)(2,1)} %get-tuple-element.5.refs_0_.refs_1_.refs_2_.refs_3_, ...), custom_call_target="tpu_custom_call" | custom-call | tf_op jit(solution)/shard_map/place/pallas_call | solution.py:731
  686.4 0.0 copy-done
  686.4 0.1 fusion
  686.5 1.1 reshape.34
  687.6 1.1 reshape.33
  (2 shorter events, 0.0 us)
Async XLA Ops:
  673.9 12.5 %copy-start = (bf16[2048,512]{1,0:T(8,128)(2,1)S(1)}, bf16[2048,512]{1,0:T(8,128)(2,1)}, u32[]{:S(2)}) copy-start(bf16[2048,512]{1,0:T(8,128)(2,1)} %get-tuple-element.6) | copy-start | bytes 6291460

commit v2 on v1

--- a/solution.py
+++ b/solution.py
@@ -15,12 +15,13 @@
 BF16 = jnp.bfloat16
 F32 = jnp.float32
 N_REL = 4
+HALVES = (0, 1)
 N_ROWCH = 4
 N_DOWN = 4
 TILE = 256
 GU_SPLIT = (0, 2, 6, 10, 14)
 MESH = pl.DeviceIdType.MESH
-VMEM_PLACE = 50331648
+VMEM_PLACE = 67043328
 
 
 def rope_freqs():
@@ -32,10 +33,14 @@
     return jnp.where(wave_len < 2048.0, inv_freq, jnp.where(wave_len > 8192.0, inv_freq / 8.0, blended))
 
 
+def upto(n):
+    return pl.ds(0, n)
+
+
 def layer_kernel(n_tp, n_fsdp, *refs):
-    (pos_ref, len_ref, freq_ref, gains, tok, wk, wv, wq, wo, wg, wu, wd,
+    (pos_ref, len_ref, freq_ref, gain_a, gain_m, tok, wk, wv, wq, wo, wg, wu, wd,
      kv_out, res, full_p, full_o, full_g, full_u, full_d, act, rs,
-     u_buf, w_buf, p_buf, x1_buf, qkv_buf, o_buf, stage, r_buf, a_stage, cos_ref, sin_ref, bias_ref,
+     u_buf, w_buf, p_buf, x1_buf, qkv_buf, o_buf, stage, r_buf, a_stage, cos_ref, sin_ref, bias_ref, gains,
      x_send, x_recv, y_send, y_recv, w_sem, wd_sem, l_sem, b_sem, a_sem, r_sem, o_sem) = refs
     n_tok, width = tok.shape
     rows = n_tok // N_ROWCH
@@ -68,84 +73,97 @@
     def al(val, mult):
         return pl.multiple_of(val, mult)
 
-    pieces = []
-
-    def add_piece(own, place):
-        pieces.append((own, place, len(pieces) % 2))
-        return len(pieces) - 1
-
-    def by_rows(full, c0, c1):
-        return lambda f: full.at[pl.ds(al(f * k_rows, k_rows), k_rows), pl.ds(c0, c1 - c0)]
+    groups = []
+
+    def add_group(pieces, area):
+        groups.append((pieces, area))
+        return len(groups) - 1
+
+    def by_rows(full, c0, n):
+        return lambda f: full.at[pl.ds(al(f * k_rows, k_rows), k_rows), pl.ds(c0, n)]
 
     def halves(own, place):
         n = own.shape[0] // 2
-        return tuple(add_piece(own.at[pl.ds(i * n, n), :], lambda f, i=i: place(f).at[pl.ds(i * n, n), :]) for i in range(2))
-
-    def cols_of(own, full, c0, c1):
-        return add_piece(own.at[:, pl.ds(c0, c1 - c0)], by_rows(full, c0, c1))
+        return [(own.at[pl.ds(i * n, n), :], lambda f, i=i: place(f).at[pl.ds(i * n, n), :], i) for i in HALVES]
+
+    def o_piece(f):
+        return full_o.at[:, pl.ds(al(f * o_cols, o_cols), o_cols)]
+
+    def d_piece(k, f):
+        return full_d.at[k, :, pl.ds(al(f * d_cols, d_cols), d_cols)]
 
     half_q = q_cols // 2
     q_from = 2 * kv_cols
-    pk = add_piece(wk, by_rows(full_p, 0, kv_cols))
-    pv = add_piece(wv, by_rows(full_p, kv_cols, q_from))
-    q0, q1 = [add_piece(wq.at[:, pl.ds(c, half_q)], by_rows(full_p, q_from + c, q_from + c + half_q)) for c in (0, half_q)]
-    po = halves(wo, lambda f: full_o.at[:, pl.ds(al(f * o_cols, o_cols), o_cols)])
-    pg = [tuple(cols_of(own, full, lo * TILE, hi * TILE) for own, full in ((wg, full_g), (wu, full_u)))
-          for lo, hi in zip(GU_SPLIT, GU_SPLIT[1:])]
-    pd = [halves(wd.at[:, pl.ds(k * d_cols, d_cols)], lambda f, k=k: full_d.at[k, :, pl.ds(al(f * d_cols, d_cols), d_cols)])
-          for k in range(N_DOWN)]
-
-    def x_copy(p, m):
-        own, place, way = pieces[p]
-        if m in (0, 1, 3):
-            src, owner = own, me_f
-        elif m == 2:
-            owner = f_left if way == 0 else f_right
+
+    def row_area(full, c0, cols):
+        return lambda n: full.at[upto(n * k_rows), pl.ds(c0, cols)]
+
+    pkv = add_group([(own, by_rows(full_p, i * kv_cols, kv_cols), i) for i, own in enumerate((wk, wv))], row_area(full_p, 0, q_from))
+    q0, q1 = [add_group([(wq.at[:, pl.ds(i * half_q, half_q)], by_rows(full_p, q_from + i * half_q, half_q), i)],
+                        row_area(full_p, q_from + i * half_q, half_q)) for i in HALVES]
+    po = add_group(halves(wo, o_piece), lambda n: full_o.at[:, upto(n * o_cols)])
+    g0, g1, g2, g3 = [
+        add_group([(own.at[:, pl.ds(lo * TILE, (hi - lo) * TILE)], by_rows(full, lo * TILE, (hi - lo) * TILE), i)
+                   for i, (own, full) in enumerate(((wg, full_g), (wu, full_u)))], row_area(full_g, 0, 2 * (hi - lo) * TILE))
+        for lo, hi in zip(GU_SPLIT, GU_SPLIT[1:])]
+    d0, d1, d2, d3 = [
+        add_group(halves(wd.at[:, pl.ds(k * d_cols, d_cols)], functools.partial(d_piece, k)), lambda n, k=k: full_d.at[k, :, upto(n * d_cols)])
+        for k in range(N_DOWN)]
+
+    FIRST, FAR_ON, TWIN = HALVES, 2, 3
+
+    def x_copy(g, i, m):
+        own, place, way = groups[g][0][i]
+        near = (f_left, f_right)
+        if m in FIRST:
+            src, owner, target = own, me_f, near[1 - m]
+        elif m == FAR_ON:
+            owner, target = near[way], near[1 - way]
             src = place(owner)
         else:
-            owner = {4: f_left, 5: f_right, 6: f_far}[m]
-            src = place(owner)
-        target = {0: f_right, 1: f_left, 2: f_right if way == 0 else f_left}.get(m, f_twin)
-        return pltpu.make_async_remote_copy(src_ref=src, dst_ref=place(owner), send_sem=x_send.at[p, m], recv_sem=x_recv.at[p, m],
+            owner, target = (me_f, f_left, f_right, f_far)[m - TWIN], f_twin
+            src = own if m == TWIN else place(owner)
+        return pltpu.make_async_remote_copy(src_ref=src, dst_ref=place(owner), send_sem=x_send.at[g], recv_sem=x_recv.at[g, min(m, TWIN)],
                                             device_id={"fsdp": target}, device_id_type=MESH)
 
-    def x_wait(p, m):
-        own, place, _ = pieces[p]
-        owner = {0: f_left, 1: f_right, 2: f_far, 3: me_f + other, 4: f_left + other, 5: f_right + other, 6: f_far + other}[m]
-        pltpu.make_async_remote_copy(src_ref=own, dst_ref=place(owner), send_sem=x_send.at[p, m], recv_sem=x_recv.at[p, m],
-                                     device_id={"fsdp": f_twin}, device_id_type=MESH).wait_recv()
-
-    def x_first(*ps):
-        for p in ps:
-            for m in (0, 1, 3):
-                x_copy(p, m).start()
-
-    def x_fwd(*ps):
-        for p in ps:
-            way = pieces[p][2]
-            x_wait(p, way)
-            x_copy(p, 2).start()
-            x_copy(p, 4 + way).start()
-
-    def x_side(*ps):
-        for p in ps:
-            way = 1 - pieces[p][2]
-            x_wait(p, way)
-            x_copy(p, 4 + way).start()
-
-    def x_second(*ps):
-        x_fwd(*ps)
-        x_side(*ps)
-
-    def x_third(*ps):
-        for p in ps:
-            x_wait(p, 2)
-            x_copy(p, 6).start()
-
-    def x_ready(*ps):
-        for p in ps:
-            for m in (3, 4, 5, 6):
-                x_wait(p, m)
+    def x_all(g, *ms):
+        for m in ms:
+            for i in range(len(groups[g][0])):
+                x_copy(g, i, m).start()
+
+    def x_taken(g, kind, n=1):
+        area = groups[g][1](n)
+        return pltpu.make_async_remote_copy(src_ref=area, dst_ref=area, send_sem=x_send.at[g], recv_sem=x_recv.at[g, kind],
+                                            device_id={"fsdp": f_twin}, device_id_type=MESH)
+
+    def x_first(*gs):
+        for g in gs:
+            x_all(g, *FIRST, TWIN)
+
+    def x_fwd(g):
+        for i, piece in enumerate(groups[g][0]):
+            x_taken(g, piece[2]).wait_recv()
+            x_copy(g, i, FAR_ON).start()
+
+    def x_side(g):
+        if len(groups[g][0]) == 1:
+            x_taken(g, 1 - groups[g][0][0][2]).wait_recv()
+        x_all(g, TWIN + 1, TWIN + 2)
+
+    def x_second(g):
+        x_fwd(g)
+        x_side(g)
+
+    def x_third(g):
+        x_taken(g, FAR_ON).wait_recv()
+        x_all(g, TWIN + 3)
+
+    def x_ready(g):
+        x_taken(g, TWIN, 4).wait_recv()
+
+    def x_sent(*gs):
+        for g in gs:
+            x_taken(g, TWIN, 7).wait_send()
 
     unit_list = [(k, pair) for pair in range(2) for k in range(N_DOWN)]
     unit_at = [2 * k + pair for k, pair in unit_list]
@@ -169,6 +187,19 @@
         return res.at[e - N_ROWCH, r]
 
     FAR, NEAR, SUM, RIGHT, LEFT, PASS = range(6)
+    OUT, SPREAD, ON = range(3)
+    sent_as = (OUT, OUT, OUT, SPREAD, SPREAD, ON)
+    GOT_FAR, GOT_SUMS, GOT_SPREAD, GOT_REST = range(4)
+
+    def got_as(e, m, h):
+        if m in (RIGHT, LEFT):
+            return GOT_SPREAD if e < N_ROWCH or m == LEFT - h else GOT_REST
+        return {FAR: GOT_FAR, PASS: GOT_REST}.get(m, GOT_SUMS)
+
+    def y_taken(e, kind, n):
+        area = rs.at[e, upto(n), :, upto(y_rows(e)[2])]
+        return pltpu.make_async_remote_copy(src_ref=area, dst_ref=area, send_sem=y_send.at[e, min(kind, ON)], recv_sem=y_recv.at[e, kind],
+                                            device_id={"tp": t_right}, device_id_type=MESH)
 
     def y_copy(e, m, h=0):
         slot, here, there = lanes(e, h)
@@ -181,50 +212,45 @@
         else:
             r, i, to = {FAR: (3, 0, h), NEAR: (1 + h, 2 - h, 1 - h), SUM: (2 - h, 1 + h, h)}[m]
             src, dst = p_buf.at[slot, pl.ds(r * sub, sub), here], rs.at[e, i, :, there]
-        return pltpu.make_async_remote_copy(src_ref=src, dst_ref=dst, send_sem=y_send.at[e, m, h], recv_sem=y_recv.at[e, m, h],
+        return pltpu.make_async_remote_copy(src_ref=src, dst_ref=dst, send_sem=y_send.at[e, sent_as[m]], recv_sem=y_recv.at[e, got_as(e, m, h)],
                                             device_id={"tp": t_right if to == 0 else t_left}, device_id_type=MESH)
 
     def rs_slice(e, i):
-        return rs.at[e, i, :, pl.ds(0, y_rows(e)[2])]
+        return rs.at[e, i, :, upto(y_rows(e)[2])]
 
     def load_stage(e, idx):
         wid = y_rows(e)[2]
         for i in idx:
-            pltpu.make_async_copy(rs_slice(e, i), stage.at[i, :, pl.ds(0, wid)], l_sem.at[i]).start()
+            pltpu.make_async_copy(rs_slice(e, i), stage.at[i, :, upto(wid)], l_sem.at[i]).start()
 
     def wait_stage(e, idx):
         wid = y_rows(e)[2]
         for i in idx:
-            pltpu.make_async_copy(rs_slice(e, i), stage.at[i, :, pl.ds(0, wid)], l_sem.at[i]).wait()
-
-    def y_start(e, hs=(0, 1)):
+            pltpu.make_async_copy(rs_slice(e, i), stage.at[i, :, upto(wid)], l_sem.at[i]).wait()
+
+    def y_start(e, hs=HALVES):
         for m in (FAR, NEAR):
             for h in hs:
                 y_copy(e, m, h).start()
 
-    def y_have(e, hs=(0, 1)):
-        for h in hs:
-            y_copy(e, NEAR, h).wait_recv()
-            y_copy(e, SUM, h).wait_recv()
-
-    def y_send_all(e, hs=(0,)):
-        for h in hs:
-            y_copy(e, LEFT, h).start()
-            y_copy(e, RIGHT, h).start()
-
-    def y_sent_all(e, hs=(0,)):
-        for h in hs:
-            y_copy(e, LEFT, h).wait_send()
-            y_copy(e, RIGHT, h).wait_send()
+    def y_have(e):
+        y_taken(e, GOT_SUMS, 2).wait_recv()
+
+    def y_send_all(e, h=0):
+        y_copy(e, LEFT, h).start()
+        y_copy(e, RIGHT, h).start()
+
+    def y_sent_all(e):
+        y_taken(e, SPREAD, 2).wait_send()
 
     EW = 32
 
     def y_add(e):
-        for h in (0, 1):
-            slot, here, there = lanes(e, h)
-            y_copy(e, FAR, h).wait_recv()
+        y_taken(e, GOT_FAR, 1).wait_recv()
+        for h in HALVES:
+            there = lanes(e, h)[2]
             pltpu.make_async_copy(rs.at[e, 0, :, there], stage.at[0, :, there], l_sem.at[h]).start()
-        for h in (0, 1):
+        for h in HALVES:
             slot, here, there = lanes(e, h)
             pltpu.make_async_copy(rs.at[e, 0, :, there], stage.at[0, :, there], l_sem.at[h]).wait()
 
@@ -269,15 +295,16 @@
         r_slot = unit_order[unit] % 2
         if unit_order[unit] >= 2:
             before = N_ROWCH + unit_at[unit_order[unit] - 2]
-            y_sent_all(before, (0, 1))
+            y_sent_all(before)
             r_out(before).wait()
-        for h in (0, 1):
+        y_have(e)
+        loads = [[pltpu.make_async_copy(rs.at[e, i, :, lanes(e, h)[2]], stage.at[i, :, lanes(e, h)[2]], l_sem.at[2 * h + i - 1])
+                  for i in (1, 2)] for h in HALVES]
+        for cp in loads[0] + loads[1]:
+            cp.start()
+        for h in HALVES:
             slot, mine, there = lanes(e, h)
-            y_have(e, (h,))
-            loads = [pltpu.make_async_copy(rs.at[e, i, :, there], stage.at[i, :, there], l_sem.at[i]) for i in (1, 2)]
-            for cp in loads:
-                cp.start()
-            for cp in loads:
+            for cp in loads[h]:
                 cp.wait()
 
             def body(i, carry, h=h, slot=slot, mine=mine):
@@ -292,39 +319,36 @@
                 return carry
 
             lax.fori_loop(0, sub // EW, body, 0)
-            y_send_all(e, (h,))
+            y_send_all(e, h)
         r_out(e).start()
 
     def r_out(e):
         return pltpu.make_async_copy(r_buf.at[unit_order[e - N_ROWCH] % 2], res.at[e - N_ROWCH, 0], r_sem.at[unit_order[e - N_ROWCH] % 2])
 
     def y_pass(e):
-        for h in (0, 1):
-            y_copy(e, LEFT - h, h if e >= N_ROWCH else 0).wait_recv()
+        y_taken(e, GOT_SPREAD, 2 if e < N_ROWCH else 1).wait_recv()
+        for h in HALVES:
             y_copy(e, PASS, h).start()
 
     def y_ready(e):
-        for h in (0, 1):
-            if e >= N_ROWCH:
-                y_copy(e, RIGHT + h, h).wait_recv()
-            y_copy(e, PASS, h).wait_recv()
+        y_taken(e, GOT_REST, 1 if e < N_ROWCH else 2).wait_recv()
 
     def bounce(src, via, dst, i):
         return pltpu.make_async_copy(src, via, b_sem.at[0, i]), pltpu.make_async_copy(via, dst, b_sem.at[1, i])
 
     small = [
-        bounce(wk, w_buf.at[0, pl.ds(0, k_rows), pl.ds(0, kv_cols)], pieces[pk][1](me_f), 0),
-        bounce(wv, w_buf.at[0, pl.ds(0, k_rows), pl.ds(kv_cols, kv_cols)], pieces[pv][1](me_f), 1),
-        bounce(wq.at[:, pl.ds(0, half_q)], w_buf.at[0, pl.ds(k_rows, k_rows), :], pieces[q0][1](me_f), 2),
-        bounce(wq.at[:, pl.ds(half_q, half_q)], w_buf.at[0, pl.ds(2 * k_rows, k_rows), :], pieces[q1][1](me_f), 3),
-        bounce(wo, w_buf.at[0, pl.ds(3 * k_rows, wo.shape[0]), :], full_o.at[:, pl.ds(al(me_f * o_cols, o_cols), o_cols)], 4),
+        bounce(wk, w_buf.at[0, upto(k_rows), upto(kv_cols)], by_rows(full_p, 0, kv_cols)(me_f), 0),
+        bounce(wv, w_buf.at[0, upto(k_rows), pl.ds(kv_cols, kv_cols)], by_rows(full_p, kv_cols, kv_cols)(me_f), 1),
+        bounce(wq.at[:, upto(half_q)], w_buf.at[0, pl.ds(k_rows, k_rows), :], by_rows(full_p, q_from, half_q)(me_f), 2),
+        bounce(wq.at[:, pl.ds(half_q, half_q)], w_buf.at[0, pl.ds(2 * k_rows, k_rows), :], by_rows(full_p, q_from + half_q, half_q)(me_f), 3),
+        bounce(wo, w_buf.at[0, pl.ds(3 * k_rows, wo.shape[0]), :], o_piece(me_f), 4),
     ] + [
-        bounce(wd.at[:, pl.ds(k * d_cols, d_cols)], w_buf.at[1, pl.ds(0, ffn), pl.ds(k * d_cols, d_cols)], full_d.at[k, :, pl.ds(al(me_f * d_cols, d_cols), d_cols)], 5 + k)
+        bounce(wd.at[:, pl.ds(k * d_cols, d_cols)], w_buf.at[1, upto(ffn), pl.ds(k * d_cols, d_cols)], d_piece(k, me_f), 5 + k)
         for k in range(N_DOWN)
     ]
     large = [
-        bounce(wg, p_buf.at[0, :, pl.ds(0, ffn)], full_g.at[pl.ds(al(me_f * k_rows, k_rows), k_rows), :], 9),
-        bounce(wu, p_buf.at[1, :, pl.ds(0, ffn)], full_u.at[pl.ds(al(me_f * k_rows, k_rows), k_rows), :], 10),
+        bounce(wg, p_buf.at[0, :, upto(ffn)], by_rows(full_g, 0, ffn)(me_f), 9),
+        bounce(wu, p_buf.at[1, :, upto(ffn)], by_rows(full_u, 0, ffn)(me_f), 10),
     ]
 
     def bounce_in(group):
@@ -378,17 +402,20 @@
         key = lax.broadcasted_iota(jnp.int32, (1, n_tok), 1)
         bias_ref[...] = jnp.where(key < len_ref[0], 0.0, -jnp.inf)
 
-    def stream(n0, n1, load, compute, hooks={}, lazy=()):
+    def stream(n0, n1, load, compute, hooks={}, lazy=(), fetched=False, then=None):
         def fetch(n, slot):
             for cp in load(n, slot):
                 cp.start()
 
-        fetch(n0, 0)
+        if not fetched:
+            fetch(n0, 0)
 
         def body(n, carry):
             slot = lax.rem(n - n0, 2)
             late = functools.reduce(jnp.logical_or, [n + 1 == at for at in lazy], n + 1 >= n1)
             pl.when(jnp.logical_not(late))(lambda: fetch(n + 1, 1 - slot))
+            if then:
+                pl.when(n + 1 == n1)(then)
             for cp in load(n, slot):
                 cp.wait()
             compute(n, slot)
@@ -404,7 +431,7 @@
 
     def project(hooks, lazy):
         def load(n, slot):
-            return (pltpu.make_async_copy(full_p.at[:, pl.ds(al(n * TILE, TILE), TILE)], w_buf.at[slot, :, pl.ds(0, TILE)], w_sem.at[slot]),)
+            return (pltpu.make_async_copy(full_p.at[:, pl.ds(al(n * TILE, TILE), TILE)], w_buf.at[slot, :, upto(TILE)], w_sem.at[slot]),)
 
         def compute(n, slot):
             plain = n == 1
@@ -497,14 +524,14 @@
         lax.fori_loop(0, n_fsdp, body, 0)
 
     def act_copy(c0, nc, n, slot):
-        return pltpu.make_async_copy(a_stage.at[slot, pl.ds(0, nc * rows), :],
+        return pltpu.make_async_copy(a_stage.at[slot, upto(nc * rows), :],
                                      act.at[pl.ds(c0 * rows, nc * rows), pl.ds(al(n * TILE, TILE), TILE)], a_sem.at[slot])
 
     def gate_up(pair, n0, n1, hooks={}):
         c0, nc = 2 * pair, 2
         def load(n, slot):
             here = pl.ds(al(n * TILE, TILE), TILE)
-            return (pltpu.make_async_copy(full_g.at[:, here], w_buf.at[slot, :, pl.ds(0, TILE)], w_sem.at[slot]),
+            return (pltpu.make_async_copy(full_g.at[:, here], w_buf.at[slot, :, upto(TILE)], w_sem.at[slot]),
                     pltpu.make_async_copy(full_u.at[:, here], w_buf.at[slot, :, pl.ds(TILE, TILE)], w_sem.at[2 + slot]))
 
         def compute(n, slot):
@@ -523,40 +550,40 @@
         for i in range(min(2, n1 - n0)):
             act_copy(c0, nc, n1 - 1, (n1 - 1 - i - n0) % 2).wait()
 
-    def load_act(pair, start=True):
-        c0, nc = 2 * pair, 2
-        cp = pltpu.make_async_copy(act.at[pl.ds(c0 * rows, nc * rows), :], u_buf.at[pl.ds(c0 * rows, nc * rows), pl.ds(0, ffn)], l_sem.at[4])
-        cp.start() if start else cp.wait()
-
-    def down(k, pair, cs):
+    def load_act(c):
+        here = pl.ds(c * rows, rows)
+        return pltpu.make_async_copy(act.at[here, :], u_buf.at[here, upto(ffn)], r_sem.at[3 + c % 2])
+
+    def down_place(slot, i):
+        return upto(ffn // 2), pl.ds(al((2 * slot + i) * TILE, TILE), TILE)
+
+    def down_tile(k, n, slot):
+        return [pltpu.make_async_copy(full_d.at[k, pl.ds(i * (ffn // 2), ffn // 2), pl.ds(al(n * TILE, TILE), TILE)],
+                                      qkv_buf.at[down_place(slot, i)], wd_sem.at[2 * slot + i]) for i in HALVES]
+
+    def down_fetch(k):
+        for cp in down_tile(k, 0, 0):
+            cp.start()
+
+    def down(k, pair, cs, fetched, then):
         e = N_ROWCH + 2 * k + pair
         slot_p, lane, _ = y_rows(e)
         half = ffn // 2
         row0, n_row = (2 * pair + cs[0]) * rows, len(cs) * rows
 
-        def place(slot, i):
-            return pl.ds(0, half), pl.ds(al((2 * slot + i) * TILE, TILE), TILE)
-
-        def load(n, slot):
-            return [pltpu.make_async_copy(full_d.at[k, pl.ds(i * half, half), pl.ds(al(n * TILE, TILE), TILE)],
-                                          qkv_buf.at[place(slot, i)], wd_sem.at[2 * slot + i]) for i in range(2)]
-
         def compute(n, slot):
-            prod = sum(jnp.dot(u_buf[row0:row0 + n_row, i * half:(i + 1) * half], qkv_buf[place(slot, i)], preferred_element_type=F32)
-                       for i in range(2)).astype(BF16)
+            prod = sum(jnp.dot(u_buf[row0:row0 + n_row, i * half:(i + 1) * half], qkv_buf[down_place(slot, i)], preferred_element_type=F32)
+                       for i in HALVES).astype(BF16)
             for i, ci in enumerate(cs):
                 p_buf[slot_p, :, pl.ds(al(lane + ci * c_cols + n * TILE, TILE), TILE)] = prod[i * rows:(i + 1) * rows, :]
 
-        stream(0, c_cols // TILE, load, compute)
+        stream(0, c_cols // TILE, functools.partial(down_tile, k), compute, fetched=fetched, then=then)
 
     def sent(e):
-        for m in (FAR, NEAR, SUM):
-            for h in (0, 1):
-                y_copy(e, m, h).wait_send()
+        y_taken(e, OUT, 3).wait_send()
 
     def passed(e):
-        for h in (0, 1):
-            y_copy(e, PASS, h).wait_send()
+        y_taken(e, ON, 1).wait_send()
 
     def scoped(fn):
         def run(*args, **kw):
@@ -567,11 +594,11 @@
     x_first, x_fwd, x_side, x_third, x_ready = map(scoped, (x_first, x_fwd, x_side, x_third, x_ready))
     y_start, y_add, y_norm, y_final, y_pass, y_ready = map(scoped, (y_start, y_add, y_norm, y_final, y_pass, y_ready))
     norm_rows, project, attend, out_project, gate_up, down = map(scoped, (norm_rows, project, attend, out_project, gate_up, down))
-    tables, bounce_in, bounce_out, bounce_end, sent, load_act = map(scoped, (tables, bounce_in, bounce_out, bounce_end, sent, load_act))
-
-    def x_done(*ps):
-        x_third(*ps)
-        x_ready(*ps)
+    tables, bounce_in, bounce_out, bounce_end, sent = map(scoped, (tables, bounce_in, bounce_out, bounce_end, sent))
+
+    def x_done(g):
+        x_third(g)
+        x_ready(g)
 
     def sent_u(*cs):
         for c in cs:
@@ -580,29 +607,34 @@
 
     c0, c1, c2, c3 = range(N_ROWCH)
     units = [N_ROWCH + u for u in unit_at]
-    g0, g1, g2, g3 = pg
-    d0, d1, d2, d3 = pd
     t0, t1, t2, t3, t4 = GU_SPLIT
 
-    def begin(i):
+    def begin(i, fetched=False, ahead=False, wait=None):
         if i >= 4:
             sent(units[i - 4])
-        parts = ((0,), (1,)) if i == 0 else ((0, 1),)
+        k, pair = unit_list[i]
+        parts = [(h,) for h in HALVES] if wait else (HALVES,)
         for cs in parts:
-            down(*unit_list[i], cs)
+            last = cs == parts[-1]
+            then = functools.partial(down_fetch, unit_list[i + 1][0]) if last and ahead else None if last else functools.partial(down_fetch, k)
+            if wait:
+                wait(cs[0])
+            down(k, pair, cs, fetched or cs != parts[0], then)
             y_start(units[i], cs)
 
-    x_first(pk, pv, q0)
+    x_first(pkv, q0)
     bounce_in(small)
-    norm_rows(lambda: x_second(pk, pv))
+    gains[:1, :] = gain_a[...].astype(F32)[None]
+    gains[1:, :] = gain_m[...].astype(F32)[None]
+    norm_rows(lambda: x_second(pkv))
     bounce_out(small)
     bounce_in(large)
     tables()
     x_fwd(q0)
     x_first(q1)
-    x_done(pk, pv)
+    x_done(pkv)
     bounce_end(small)
-    kv_copy = pltpu.make_async_copy(qkv_buf.at[:, pl.ds(0, q_from)], kv_out, r_sem.at[2])
+    kv_copy = pltpu.make_async_copy(qkv_buf.at[:, upto(q_from)], kv_out, r_sem.at[2])
 
     def have_kv():
         bounce_out(large)
@@ -611,13 +643,13 @@
         x_done(q0)
 
     project({
-        0: lambda: (x_fwd(q1), x_first(*po)),
+        0: lambda: (x_fwd(q1), x_first(po)),
         1: have_kv,
         3: lambda: (x_side(q1), x_done(q1)),
-        4: lambda: (x_second(*po), x_first(*g0, *g1, *g2)),
+        4: lambda: (x_second(po), x_first(g0, g1, g2)),
     }, (2, 4))
     attend(c0)
-    x_done(*po)
+    x_done(po)
     out_load()
     bounce_end(large)
     out_project(c0)
@@ -625,10 +657,10 @@
     attend(c1)
     out_project(c1)
     y_start(c1)
-    x_second(*g0)
+    x_second(g0)
     attend(c2, lambda: y_add(c0))
     attend(c3, lambda: y_add(c1))
-    x_second(*g1)
+    x_second(g1)
     y_norm(c0)
     y_norm(c1)
     sent(c0)
@@ -639,79 +671,84 @@
     y_pass(c1)
     y_start(c2)
     y_start(c3)
-    x_second(*g2)
-    x_first(*g3)
-    x_third(*g0)
-    x_third(*g1)
-    x_ready(*g0)
+    x_second(g2)
+    x_first(g3)
+    x_third(g0)
+    x_third(g1)
+    x_ready(g0)
     y_ready(c0)
     y_ready(c1)
-    x_ready(*g1)
-    gate_up(0, t0, t3, {t1: lambda: (x_third(*g2), y_add(c2)), t2 - 2: lambda: x_ready(*g2), t2 + 1: lambda: y_add(c3)})
-    x_second(*g3)
-    x_first(*d0)
+    x_ready(g1)
+    gate_up(0, t0, t3, {t1: lambda: (x_third(g2), y_add(c2)), t2 - 2: lambda: x_ready(g2), t2 + 1: lambda: y_add(c3)})
+    x_second(g3)
+    x_first(d0)
     y_norm(c2)
     y_norm(c3)
-    x_done(*g3)
+    x_done(g3)
     y_pass(c2)
-    gate_up(0, t3, t4, {t3 + 1: lambda: (x_second(*d0), x_first(*d1)), t4 - 2: lambda: y_pass(c3)})
+    gate_up(0, t3, t4, {t3 + 1: lambda: (x_second(d0), x_first(d1)), t4 - 2: lambda: y_pass(c3)})
     sent_u(c0, c1)
-    load_act(0)
-    x_done(*d0)
-    load_act(0, False)
+    load_act(c0).start()
+    load_act(c1).start()
     kv_copy.wait()
+    x_done(d0)
+    down_fetch(0)
     sent(c2)
     sent(c3)
-    begin(0)
-    x_second(*d1)
-    x_first(*d2)
+    (load_act(c0).wait(), load_act(c1).wait(), begin(0, True))
+    x_second(d1)
+    x_first(d2)
     y_ready(c2)
     y_ready(c3)
     sent_u(c2, c3)
     f0, f1, f2, f3 = units[:N_DOWN]
     gate_up(1, t0, t4, {
-        1: lambda: (y_add(f0), x_done(*d1), begin(1)),
+        1: lambda: (y_add(f0), x_done(d1), begin(1)),
         2: lambda: y_final(*unit_list[0]),
-        3: lambda: (x_second(*d2), x_first(*d3)),
+        3: lambda: (x_second(d2), x_first(d3)),
         4: lambda: y_add(f1),
-        5: lambda: (y_pass(f0), x_third(*d2)),
-        6: lambda: (y_final(*unit_list[1]), x_ready(*d2), begin(2)),
-        7: lambda: x_second(*d3),
+        5: lambda: (y_pass(f0), x_third(d2)),
+        6: lambda: (y_final(*unit_list[1]), x_ready(d2), begin(2)),
+        7: lambda: x_second(d3),
         8: lambda: y_pass(f1),
-        9: lambda: (y_add(f2), x_done(*d3), begin(3)),
+        9: lambda: (y_add(f2), x_done(d3), begin(3)),
         10: lambda: y_final(*unit_list[2]),
-        12: lambda: y_add(f3),
+        12: lambda: (y_add(f3), down_fetch(0)),
     })
-    load_act(1)
+    load_act(c2).start()
+    load_act(c3).start()
     y_pass(f2)
-    load_act(1, False)
     n_unit = len(units)
     half = n_unit // 2
-    begin(half)
+    begin(half, True, True, lambda h: load_act(2 + h).wait())
     y_final(*unit_list[half - 1])
     for i in range(half, n_unit):
         if i + 1 < n_unit:
-            begin(i + 1)
+            begin(i + 1, True, i + 2 < n_unit)
         y_add(units[i])
+        x_sent(*range(len(groups) * (i - half) // half, len(groups) * (i + 1 - half) // half))
         y_pass(units[i - 1])
+        if i > half:
+            y_ready(units[i - 2])
+            passed(units[i - 2])
         y_final(*unit_list[i])
+    for e in units[-4:]:
+        sent(e)
     y_pass(units[-1])
-
-    for e in units:
+    for e in units[:half - 1] + units[-2:]:
         y_ready(e)
         passed(e)
-    for e in units[-4:]:
-        sent(e)
     for e in units[-2:]:
-        y_sent_all(e, (0, 1))
+        y_sent_all(e)
         r_out(e).wait()
-    for p in range(len(pieces)):
-        for m in range(7):
-            x_copy(p, m).wait_send()
 
 
 def place_kernel(n_tp, n_fsdp, *refs):
-    srcs, out_ref = refs[:N_DOWN], refs[N_DOWN]
+    srcs, kv_ref = refs[:N_DOWN], refs[N_DOWN]
+    out_ref, *cache_refs = refs[N_DOWN + 1:]
+    for i, cache in enumerate(cache_refs):
+        cols = cache.shape[1] * cache.shape[2]
+        cache[...] = kv_ref[:, i * cols:(i + 1) * cols].reshape(cache.shape)
     sub = srcs[0].shape[2]
     cols = srcs[0].shape[3] // n_fsdp
     for r, dist in enumerate((0, n_tp - 1, 1, 2)):
@@ -722,7 +759,10 @@
                 out_ref[here, c0:c0 + cols] = srcs[k][0, r, :, f * cols:(f + 1) * cols]
 
 
-def place(res, n_tok, width, n_tp, n_fsdp):
+def place(res, kv_all, n_tok, width, n_tp, n_fsdp):
+    rows, kv_cols = n_tok // N_ROWCH, kv_all.shape[1]
+    n_kv = kv_cols // 2 // HEAD_DIM
+    cache = jax.ShapeDtypeStruct((n_tok, n_kv, HEAD_DIM), BF16)
     sub, c_cols = res.shape[2], res.shape[3] // 2
 
     def src_spec(k):
@@ -730,13 +770,13 @@
 
     return pl.pallas_call(
         functools.partial(place_kernel, n_tp, n_fsdp),
-        out_shape=jax.ShapeDtypeStruct((n_tok, width), BF16),
+        out_shape=[jax.ShapeDtypeStruct((n_tok, width), BF16), cache, cache],
         grid=(N_ROWCH,),
-        in_specs=[src_spec(k) for k in range(N_DOWN)],
-        out_specs=pl.BlockSpec((N_REL * sub, width), lambda c: (c, 0)),
+        in_specs=[src_spec(k) for k in range(N_DOWN)] + [pl.BlockSpec((rows, kv_cols), lambda c: (c, 0))],
+        out_specs=[pl.BlockSpec((rows, width), lambda c: (c, 0))] + [pl.BlockSpec((rows, n_kv, HEAD_DIM), lambda c: (c, 0, 0))] * 2,
         compiler_params=pltpu.CompilerParams(vmem_limit_bytes=VMEM_PLACE),
         name="place",
-    )(*([res] * N_DOWN))
+    )(*([res] * N_DOWN), kv_all)
 
 
 def solution(mesh):
@@ -756,11 +796,10 @@
         c_cols = width // N_DOWN
         n_units = 2 * N_DOWN
         freqs = jnp.tile(rope_freqs(), 2)[None]
-        gains = jnp.stack([norm_attn, norm_mlp]).astype(F32)
         vm = pl.BlockSpec(memory_space=pltpu.VMEM)
         smem = pl.BlockSpec(memory_space=pltpu.SMEM)
         hbm = pl.BlockSpec(memory_space=pl.ANY)
-        n_pieces = 6 + 2 * (len(GU_SPLIT) - 1 + N_DOWN)
+        n_groups = 4 + len(GU_SPLIT) - 1 + N_DOWN
         n_y = N_ROWCH + n_units
         st = lambda *s: jax.ShapeDtypeStruct(s, BF16)
         dma = pltpu.SemaphoreType.DMA
@@ -769,7 +808,7 @@
             out_shape=[st(n_tok, 2 * kv_cols), st(n_units, N_REL, sub, 2 * c_cols),
                        st(width, 2 * kv_cols + q_cols), st(w_out.shape[0], width),
                        st(width, ffn), st(width, ffn), st(N_DOWN, ffn, c_cols), st(n_tok, ffn), st(n_y, 3, sub, width)],
-            in_specs=[smem] * 2 + [vm] * 2 + [hbm] * 8,
+            in_specs=[smem] * 2 + [vm] * 3 + [hbm] * 8,
             out_specs=[hbm] * 9,
             scratch_shapes=[
                 pltpu.VMEM((n_tok, width), BF16), pltpu.VMEM((2, width, 2 * TILE), BF16),
@@ -778,18 +817,16 @@
                 pltpu.VMEM((2, rows, q_cols), BF16), pltpu.VMEM((3, sub, width), BF16),
                 pltpu.VMEM((2, sub, 2 * c_cols), BF16), pltpu.VMEM((2, 2 * rows, TILE), BF16),
                 pltpu.VMEM((n_tok, HEAD_DIM), F32), pltpu.VMEM((n_tok, HEAD_DIM), F32), pltpu.VMEM((1, n_tok), F32),
-                dma((n_pieces, 7)), dma((n_pieces, 7)), dma((n_y, 6, 2)), dma((n_y, 6, 2)),
-                dma((4,)), dma((4,)), dma((5,)), dma((2, 11)), dma((2,)), dma((3,)), dma((n_fsdp,)),
+                pltpu.VMEM((2, width), F32),
+                dma((n_groups,)), dma((n_groups, 4)), dma((n_y, 3)), dma((n_y, 4)),
+                dma((4,)), dma((4,)), dma((5,)), dma((2, 11)), dma((2,)), dma((5,)), dma((n_fsdp,)),
             ],
             compiler_params=pltpu.CompilerParams(vmem_limit_bytes=67043328, collective_id=0, has_side_effects=True),
             name="layer",
-        )(positions, valid_len, freqs, gains, tokens[0],
+        )(positions, valid_len, freqs, norm_attn, norm_mlp, tokens[0],
           w_key, w_value, w_query, w_out, w_gate, w_up, w_down)
         kv_all, res = outs[0], outs[1]
-        hidden = place(res, n_tok, width, n_tp, n_fsdp)
-        n_kv = kv_cols // HEAD_DIM
-        key_cache = kv_all[:, :kv_cols].reshape(1, n_tok, n_kv, HEAD_DIM)
-        value_cache = kv_all[:, kv_cols:].reshape(1, n_tok, n_kv, HEAD_DIM)
-        return hidden[None], key_cache, value_cache
+        hidden, key_cache, value_cache = place(res, kv_all, n_tok, width, n_tp, n_fsdp)
+        return hidden[None], key_cache[None], value_cache[None]
 
     return jax.shard_map(local_layer, mesh=mesh, in_specs=in_specs, out_specs=out_specs, check_vma=False)

time: 691 us -> 681 us (0.986)
  no operation moved by 1% of the time
where the time goes in v2:
time: 681 us; the launch traced here: 679 us
  Pallas kernels  677 us (99%)
    pallas_call x1, Pallas kernels, local_layer(): pl.pallas_call(functools.partial(layer_kernel, n_tp, n_fsdp), out_shape=[...  664 us

profile of v2, /device:TPU:96, one launch (start us, length us, event | category | flops | bytes accessed | tf_op | source)
XLA Modules:
  0.0 679.2 jit_solution(5975698253650643443)
XLA Ops:
  1.3 0.6 broadcast_in_dim_tile.3.refs_2_
  1.9 664.0 %layer.1 = (bf16[2048,512]{1,0:T(8,128)(2,1)}, bf16[8,4,128,2048]{3,2,1,0:T(8,128)(2,1)}, bf16[4096,1536]{1,0:T(8,128)(2,1)}, bf16[1024,4096]{1,0:T(8,128)(2,1)}...) custom-call(s32[1,2048]{1,0:T(1,128)} %refs_0_.1, ...), custom_call_target="tpu_custom_call" | custom-call | tf_op jit(solution)/shard_map/layer/pallas_call | solution.py:806
  665.9 13.4 %place.1 = (bf16[2048,4096]{1,0:T(8,128)(2,1)}, bf16[2048,2,128]{2,1,0:T(2,128)(2,1)}, bf16[2048,2,128]{2,1,0:T(2,128)(2,1)}) custom-call(bf16[8,4,128,2048]{3,2,1,0:T(8,128)(2,1)} %get-tuple-element.8.refs_0_.refs_1_.refs_2_.refs_3_, bf16[8,4,128,2048]{3,2,1,0:T(8,128)(2,1)} %get-tuple-element.8.refs_0_.refs_1_.refs_2_.refs_3_, ...), custom_call_target="tpu_custom_call" | custom-call | tf_op jit(solution)/shard_map/place/pallas_call | solution.py:771
  (2 shorter events, 0.0 us)

commit v3 on v2

--- a/solution.py
+++ b/solution.py
@@ -236,9 +236,9 @@
     def y_have(e):
         y_taken(e, GOT_SUMS, 2).wait_recv()
 
-    def y_send_all(e, h=0):
-        y_copy(e, LEFT, h).start()
-        y_copy(e, RIGHT, h).start()
+    def y_send_all(e):
+        y_copy(e, LEFT).start()
+        y_copy(e, RIGHT).start()
 
     def y_sent_all(e):
         y_taken(e, SPREAD, 2).wait_send()
@@ -319,7 +319,8 @@
                 return carry
 
             lax.fori_loop(0, sub // EW, body, 0)
-            y_send_all(e, h)
+        for m, h in ((LEFT, 0), (RIGHT, 1), (LEFT, 1), (RIGHT, 0)):
+            y_copy(e, m, h).start()
         r_out(e).start()
 
     def r_out(e):
@@ -707,9 +708,8 @@
         2: lambda: y_final(*unit_list[0]),
         3: lambda: (x_second(d2), x_first(d3)),
         4: lambda: y_add(f1),
-        5: lambda: (y_pass(f0), x_third(d2)),
-        6: lambda: (y_final(*unit_list[1]), x_ready(d2), begin(2)),
-        7: lambda: x_second(d3),
+        5: lambda: x_third(d2),
+        6: lambda: (y_pass(f0), y_final(*unit_list[1]), x_ready(d2), begin(2), x_second(d3)),
         8: lambda: y_pass(f1),
         9: lambda: (y_add(f2), x_done(d3), begin(3)),
         10: lambda: y_final(*unit_list[2]),
@@ -725,12 +725,15 @@
     for i in range(half, n_unit):
         if i + 1 < n_unit:
             begin(i + 1, True, i + 2 < n_unit)
-        y_add(units[i])
+        if i == half:
+            y_add(units[i])
         x_sent(*range(len(groups) * (i - half) // half, len(groups) * (i + 1 - half) // half))
         y_pass(units[i - 1])
         if i > half:
             y_ready(units[i - 2])
             passed(units[i - 2])
+        if i + 1 < n_unit:
+            y_add(units[i + 1])
         y_final(*unit_list[i])
     for e in units[-4:]:
         sent(e)
@@ -743,40 +746,75 @@
         r_out(e).wait()
 
 
-def place_kernel(n_tp, n_fsdp, *refs):
-    srcs, kv_ref = refs[:N_DOWN], refs[N_DOWN]
-    out_ref, *cache_refs = refs[N_DOWN + 1:]
-    for i, cache in enumerate(cache_refs):
-        cols = cache.shape[1] * cache.shape[2]
-        cache[...] = kv_ref[:, i * cols:(i + 1) * cols].reshape(cache.shape)
-    sub = srcs[0].shape[2]
-    cols = srcs[0].shape[3] // n_fsdp
-    for r, dist in enumerate((0, n_tp - 1, 1, 2)):
-        here = pl.ds(pl.multiple_of(lax.rem(lax.axis_index("tp") + dist, n_tp) * sub, sub), sub)
+def place_kernel(n_tp, n_fsdp, res, kv, out, key_out, value_out, in_buf, out_buf, kv_buf, cache_buf, in_sem, out_sem, kv_sem, cache_sem):
+    sub, c_cols = res.shape[2], res.shape[3] // 2
+    cols = c_cols // n_fsdp
+    me_t = lax.axis_index("tp")
+
+    def load(c, k):
+        src = res.at[2 * k + c // 2, :, :, pl.ds(pl.multiple_of(lax.rem(c, 2) * c_cols, c_cols), c_cols)]
+        return pltpu.make_async_copy(src, in_buf.at[c, k], in_sem.at[c])
+
+    def store(c, r):
+        here = pl.ds(pl.multiple_of((c * N_REL + r) * sub, sub), sub)
+        return pltpu.make_async_copy(out_buf.at[here, :], out.at[here, :], out_sem.at[c, r])
+
+    def caches():
+        return [pltpu.make_async_copy(cache_buf.at[i], dst, cache_sem.at[i]) for i, dst in enumerate((key_out, value_out))]
+
+    for c in range(N_ROWCH):
         for k in range(N_DOWN):
-            for f in range(n_fsdp):
-                c0 = (f * N_DOWN + k) * cols
-                out_ref[here, c0:c0 + cols] = srcs[k][0, r, :, f * cols:(f + 1) * cols]
+            load(c, k).start()
+    kv_load = pltpu.make_async_copy(kv, kv_buf, kv_sem)
+    kv_load.start()
+
+    def chunk(c, carry):
+        pltpu.make_async_copy(res.at[upto(N_DOWN), :, :, upto(c_cols)], in_buf.at[c], in_sem.at[c]).wait()
+        for r, dist in enumerate((0, n_tp - 1, 1, 2)):
+            row = lax.rem(me_t + dist, n_tp)
+            here = pl.ds(pl.multiple_of((c * N_REL + row) * sub, sub), sub)
+            for k in range(N_DOWN):
+                for f in range(n_fsdp):
+                    c0 = (f * N_DOWN + k) * cols
+                    out_buf[here, c0:c0 + cols] = in_buf[c, k, r, :, f * cols:(f + 1) * cols]
+            store(c, row).start()
+        return carry
+
+    lax.fori_loop(0, N_ROWCH, chunk, 0)
+    kv_load.wait()
+    for i in HALVES:
+        n = kv.shape[1] // 2
+        cache_buf[i] = kv_buf[:, i * n:(i + 1) * n].reshape(cache_buf.shape[1:])
+    for cp in caches():
+        cp.start()
+
+    def finish(c, carry):
+        for r in range(N_REL):
+            store(c, r).wait()
+        return carry
+
+    lax.fori_loop(0, N_ROWCH, finish, 0)
+    for cp in caches():
+        cp.wait()
 
 
 def place(res, kv_all, n_tok, width, n_tp, n_fsdp):
-    rows, kv_cols = n_tok // N_ROWCH, kv_all.shape[1]
-    n_kv = kv_cols // 2 // HEAD_DIM
-    cache = jax.ShapeDtypeStruct((n_tok, n_kv, HEAD_DIM), BF16)
     sub, c_cols = res.shape[2], res.shape[3] // 2
-
-    def src_spec(k):
-        return pl.BlockSpec((1, N_REL, sub, c_cols), lambda c: (2 * k + c // 2, 0, 0, c % 2))
-
+    kv_cols = kv_all.shape[1]
+    cache = (n_tok, kv_cols // 2 // HEAD_DIM, HEAD_DIM)
+    hbm = pl.BlockSpec(memory_space=pl.ANY)
+    dma = pltpu.SemaphoreType.DMA
     return pl.pallas_call(
         functools.partial(place_kernel, n_tp, n_fsdp),
-        out_shape=[jax.ShapeDtypeStruct((n_tok, width), BF16), cache, cache],
-        grid=(N_ROWCH,),
-        in_specs=[src_spec(k) for k in range(N_DOWN)] + [pl.BlockSpec((rows, kv_cols), lambda c: (c, 0))],
-        out_specs=[pl.BlockSpec((rows, width), lambda c: (c, 0))] + [pl.BlockSpec((rows, n_kv, HEAD_DIM), lambda c: (c, 0, 0))] * 2,
+        out_shape=[jax.ShapeDtypeStruct((n_tok, width), BF16)] + [jax.ShapeDtypeStruct(cache, BF16)] * 2,
+        in_specs=[hbm] * 2,
+        out_specs=[hbm] * 3,
+        scratch_shapes=[pltpu.VMEM((N_ROWCH, N_DOWN, N_REL, sub, c_cols), BF16), pltpu.VMEM((n_tok, width), BF16),
+                        pltpu.VMEM((n_tok, kv_cols), BF16), pltpu.VMEM((2, *cache), BF16),
+                        dma((N_ROWCH,)), dma((N_ROWCH, N_REL)), dma, dma((2,))],
         compiler_params=pltpu.CompilerParams(vmem_limit_bytes=VMEM_PLACE),
         name="place",
-    )(*([res] * N_DOWN), kv_all)
+    )(res, kv_all)
 
 
 def solution(mesh):

time: 681 us -> 680 us (level)
  no operation moved by 1% of the time
where the time goes in v3:
time: 680 us; the launch traced here: 679 us
  Pallas kernels  676 us (99%)
    pallas_call x1, Pallas kernels, local_layer(): pl.pallas_call(functools.partial(layer_kernel, n_tp, n_fsdp), out_shape=[...  664 us

profile of v3, /device:TPU:96, one launch (start us, length us, event | category | flops | bytes accessed | tf_op | source)
XLA Modules:
  0.0 678.6 jit_solution(7025570265923527633)
XLA Ops:
  1.3 0.6 broadcast_in_dim_tile.3.refs_2_
  1.9 663.8 %layer.1 = (bf16[2048,512]{1,0:T(8,128)(2,1)}, bf16[8,4,128,2048]{3,2,1,0:T(8,128)(2,1)}, bf16[4096,1536]{1,0:T(8,128)(2,1)}, bf16[1024,4096]{1,0:T(8,128)(2,1)}...) custom-call(s32[1,2048]{1,0:T(1,128)} %refs_0_.1, ...), custom_call_target="tpu_custom_call" | custom-call | tf_op jit(solution)/shard_map/layer/pallas_call | solution.py:844
  665.7 12.7 %place.1 = (bf16[2048,4096]{1,0:T(8,128)(2,1)}, bf16[2048,2,128]{2,1,0:T(2,128)(2,1)}, bf16[2048,2,128]{2,1,0:T(2,128)(2,1)}) custom-call(bf16[8,4,128,2048]{3,2,1,0:T(8,128)(2,1)} %get-tuple-element.8.res, bf16[2048,512]{1,0:T(8,128)(2,1)} %get-tuple-element.9.kv), custom_call_target="tpu_custom_call" | custom-call | tf_op jit(solution)/shard_map/place/pallas_call | solution.py:807
  (2 shorter events, 0.0 us)

commit v4 on v3

--- a/solution.py
+++ b/solution.py
@@ -335,7 +335,7 @@
         y_taken(e, GOT_REST, 1 if e < N_ROWCH else 2).wait_recv()
 
     def bounce(src, via, dst, i):
-        return pltpu.make_async_copy(src, via, b_sem.at[0, i]), pltpu.make_async_copy(via, dst, b_sem.at[1, i])
+        return pltpu.make_async_copy(src, via, b_sem.at[i]), pltpu.make_async_copy(via, dst, b_sem.at[i])
 
     small = [
         bounce(wk, w_buf.at[0, upto(k_rows), upto(kv_cols)], by_rows(full_p, 0, kv_cols)(me_f), 0),
@@ -704,10 +704,8 @@
     sent_u(c2, c3)
     f0, f1, f2, f3 = units[:N_DOWN]
     gate_up(1, t0, t4, {
-        1: lambda: (y_add(f0), x_done(d1), begin(1)),
-        2: lambda: y_final(*unit_list[0]),
-        3: lambda: (x_second(d2), x_first(d3)),
-        4: lambda: y_add(f1),
+        1: lambda: (y_add(f0), x_done(d1), begin(1), y_final(*unit_list[0])),
+        3: lambda: (y_add(f1), x_second(d2), x_first(d3)),
         5: lambda: x_third(d2),
         6: lambda: (y_pass(f0), y_final(*unit_list[1]), x_ready(d2), begin(2), x_second(d3)),
         8: lambda: y_pass(f1),
@@ -857,7 +855,7 @@
                 pltpu.VMEM((n_tok, HEAD_DIM), F32), pltpu.VMEM((n_tok, HEAD_DIM), F32), pltpu.VMEM((1, n_tok), F32),
                 pltpu.VMEM((2, width), F32),
                 dma((n_groups,)), dma((n_groups, 4)), dma((n_y, 3)), dma((n_y, 4)),
-                dma((4,)), dma((4,)), dma((5,)), dma((2, 11)), dma((2,)), dma((5,)), dma((n_fsdp,)),
+                dma((4,)), dma((4,)), dma((5,)), dma((11,)), dma((2,)), dma((5,)), dma((n_fsdp,)),
             ],
             compiler_params=pltpu.CompilerParams(vmem_limit_bytes=67043328, collective_id=0, has_side_effects=True),
             name="layer",

time: 680 us -> 679 us (level)
  no operation moved by 1% of the time
where the time goes in v4:
time: 679 us; the launch traced here: 678 us
  Pallas kernels  676 us (100%)
    pallas_call x1, Pallas kernels, local_layer(): pl.pallas_call(functools.partial(layer_kernel, n_tp, n_fsdp), out_shape=[...  664 us

profile of v4, /device:TPU:96, one launch (start us, length us, event | category | flops | bytes accessed | tf_op | source)
XLA Modules:
  0.0 678.4 jit_solution(7412444253211031625)
XLA Ops:
  1.3 0.6 broadcast_in_dim_tile.3.refs_2_
  1.9 663.6 %layer.1 = (bf16[2048,512]{1,0:T(8,128)(2,1)}, bf16[8,4,128,2048]{3,2,1,0:T(8,128)(2,1)}, bf16[4096,1536]{1,0:T(8,128)(2,1)}, bf16[1024,4096]{1,0:T(8,128)(2,1)}...) custom-call(s32[1,2048]{1,0:T(1,128)} %refs_0_.1, ...), custom_call_target="tpu_custom_call" | custom-call | tf_op jit(solution)/shard_map/layer/pallas_call | solution.py:842
  665.6 12.7 %place.1 = (bf16[2048,4096]{1,0:T(8,128)(2,1)}, bf16[2048,2,128]{2,1,0:T(2,128)(2,1)}, bf16[2048,2,128]{2,1,0:T(2,128)(2,1)}) custom-call(bf16[8,4,128,2048]{3,2,1,0:T(8,128)(2,1)} %get-tuple-element.8.res, bf16[2048,512]{1,0:T(8,128)(2,1)} %get-tuple-element.9.kv), custom_call_target="tpu_custom_call" | custom-call | tf_op jit(solution)/shard_map/place/pallas_call | solution.py:805
  (2 shorter events, 0.0 us)
